TPU v7x, 128 devices: a whole 4x4x4 slice. The times are simulated.
128 devices in a mesh: dp: 32 (over x, z_lo, y), expert: 4 (over z_hi, core).
Axes of the slice: x: 4, y: 4, z: 4 (z_hi: 2, z_lo: 2; z = z_hi * 2 + z_lo), core: 2. Of those that a mesh axis runs over, the one named last changes fastest.
Arguments:
- cotangent: bfloat16 [131072, 2048], P(('dp', 'expert')), may hold values from -6 to 6
- route_ids: int32 [131072, 6], P(('dp', 'expert')), may hold values from 0 to 63, all different within a row; in each aligned block of 1024 rows (0 to 1023, 1024 to 2047, ...) at most 192 rows name the same one
- route_weights: float32 [131072, 6], P(('dp', 'expert')), may hold values from 0.02 to 1
- hidden: bfloat16 [8, 24576, 1408], P('expert', 'dp'), may hold values from -6 to 6
- master: float32 [1408, 8, 2048], P('dp', 'expert'), may hold values from -0.3 to 0.3
- first_moment: float32 [1408, 8, 2048], P('dp', 'expert'), may hold values from -1.2 to 1.2
- second_moment: float32 [1408, 8, 2048], P('dp', 'expert'), may hold values from 0.002 to 0.05
Outputs:
- new_master: float32 [1408, 8, 2048], P('dp', 'expert')
- new_first: float32 [1408, 8, 2048], P('dp', 'expert')
- new_second: float32 [1408, 8, 2048], P('dp', 'expert')
Inputs may be any that keep to these rules, and one draw needn't show every extreme that they name: `route_ids`: each row names 6 different experts. Within the 1024 rows of one device no expert is named by more than 192 rows.
All inputs are finite; a program needn't handle non-finite values.
Results may differ from a plain program's by a relative error of at most 0.0019.
Values may be sent and summed in bfloat16 or wider, within the bound.
No kernel may reach another device: no remote copies, remote signals or barrier semaphores. Data moves between devices by JAX's collectives and lax.ppermute only.
A program may use at most 128 MiB of HBM per device.

v0:
```python
import functools

import jax
import jax.numpy as jnp
from jax import lax
from jax.experimental import pallas as pl
from jax.experimental.layout import Layout, with_layout_constraint
from jax.experimental.pallas import tpu as pltpu
from jax.sharding import PartitionSpec as P


beta_one = 0.9
beta_two = 0.999
learning_rate = 0.001
epsilon = 1e-08
decay_rate = 0.1
step_count = 4.0

GROUPS = ((768,), (896, 384))
WAVES = ((0, 1), (2,))
RINGS = (True, True, False)
ROW_MAJOR = Layout(major_to_minor=(0, 1, 2))
WIDE, NARROW = 60 * 1024 * 2**10, 24 * 2**20
AXES = ("dp", "expert")


def device_of(x, y, z, core):
    return (x % 4 * 8 + z % 2 * 4 + y % 4) * 4 + z // 2 * 2 + core


def moves(step):
    pairs = []
    for x in range(4):
        for y in range(4):
            for z in range(4):
                for core in range(2):
                    pairs.append((device_of(x, y, z, core), device_of(*step(x, y, z, core))))
    return pairs


ALONG_X = {j: moves(lambda x, y, z, core, j=j: (x + j, y, z, core)) for j in (1, 2, 3)}
ALONG_Y = {j: moves(lambda x, y, z, core, j=j: (x, y + j, z, core)) for j in (1, 2, 3)}
PAIR_Z = moves(lambda x, y, z, core: (x, y, z ^ 1, core))
TO_EXPERT = {
    m: moves(lambda x, y, z, core, m=m: (x, y, z ^ (m & 2), core ^ (m & 1))) for m in (1, 2, 3)
}


def send(array, pairs):
    return lax.ppermute(array, AXES, pairs)


def dispatch_body(start, own_ref, ids_hbm, weights_hbm, cot_hbm, *refs):
    out_refs, (ids_ref, weights_ref, cot_ref, sems) = refs[:-4], refs[-4:]
    capacity = out_refs[0].shape[1]
    tokens, part = cot_ref.shape
    columns = cot_hbm.at[:, pl.ds(start, part)]
    pairs = ((ids_hbm, ids_ref), (weights_hbm, weights_ref), (columns, cot_ref))
    copies = [pltpu.make_async_copy(a, b, sems.at[n]) for n, (a, b) in enumerate(pairs)]
    for copy in copies:
        copy.start()
    own = own_ref[0]
    copies[0].wait()
    copies[1].wait()
    ids = ids_ref[...]
    weights = weights_ref[...]
    chosen, weight_rows = [], []
    for m in range(4):
        for local in range(2):
            match = ids == 2 * jnp.bitwise_xor(own, m) + local
            chosen.append(jnp.sum(match.astype(jnp.float32), axis=0, keepdims=True))
            weight_rows.append(jnp.sum(jnp.where(match, weights, 0.0), axis=0, keepdims=True))
    taken = jnp.concatenate(chosen, axis=0)
    ahead = lax.broadcasted_iota(jnp.int32, (128, 128), 0) < lax.broadcasted_iota(
        jnp.int32, (128, 128), 1
    )
    ahead = ahead.astype(jnp.float32).astype(jnp.bfloat16)
    offset = jnp.zeros((8, 1), jnp.float32)
    ranks = []
    for start in range(0, tokens, 128):
        tile = taken[:, start : start + 128]
        inside = jnp.dot(tile.astype(jnp.bfloat16), ahead, preferred_element_type=jnp.float32)
        ranks.append(jnp.where(tile > 0.0, inside + offset, -1.0))
        offset = offset + jnp.sum(tile, axis=1, keepdims=True)
    rank = jnp.concatenate(ranks, axis=1).astype(jnp.int32)
    slot = lax.broadcasted_iota(jnp.int32, (capacity, tokens), 0)
    far = (len(out_refs) - 2) // 2
    copies[2].wait()
    for m in (2, 3, 1, 0):
        for local in range(2):
            k = 2 * m + local
            mask = rank[k : k + 1, :] == slot
            picked = jnp.dot(
                jnp.where(mask, 1.0, 0.0).astype(jnp.bfloat16),
                cot_ref[...],
                preferred_element_type=jnp.float32,
            )
            weight = jnp.sum(jnp.where(mask, weight_rows[k], 0.0), axis=1, keepdims=True)
            rows = (picked * weight).astype(jnp.bfloat16)
            if m < 2:
                out_refs[m][local] = rows
            else:
                at = 0
                for out in out_refs[2 + far * (m - 2) : 2 + far * (m - 1)]:
                    out[local] = rows[:, at : at + out.shape[2]]
                    at += out.shape[2]


def dispatch(own, ids, weights, cotangent, widths, start, capacity):
    tokens = cotangent.shape[0]
    part = sum(widths)
    whole = lambda shape: pl.BlockSpec(shape, lambda i, s: (0,) * len(shape))
    shapes = [(2, capacity, part)] * 2 + [(2, capacity, w) for w in widths] * 2
    outs = pl.pallas_call(
        functools.partial(dispatch_body, start),
        grid_spec=pltpu.PrefetchScalarGridSpec(
            num_scalar_prefetch=1,
            grid=(1,),
            in_specs=[pl.BlockSpec(memory_space=pltpu.HBM)] * 3,
            out_specs=[whole(shape) for shape in shapes],
            scratch_shapes=[
                pltpu.VMEM(ids.shape, ids.dtype),
                pltpu.VMEM(weights.shape, weights.dtype),
                pltpu.VMEM((tokens, part), cotangent.dtype),
                pltpu.SemaphoreType.DMA((3,)),
            ],
        ),
        out_shape=[jax.ShapeDtypeStruct(shape, jnp.bfloat16) for shape in shapes],
        compiler_params=pltpu.CompilerParams(vmem_limit_bytes=WIDE if start == 0 else NARROW),
    )(own, ids, weights, cotangent)
    n = len(widths)
    return outs[0], outs[1], outs[2 : 2 + n], outs[2 + n :]


def prepare_body(place_ref, hidden_hbm, out_ref, hidden_ref, sems):
    local, block = pl.program_id(0), pl.program_id(1)

    def copy(n):
        return pltpu.make_async_copy(hidden_hbm.at[n], hidden_ref.at[n], sems.at[n])

    @pl.when((local == 0) & (block == 0))
    def fetch():
        copy(0).start()
        copy(1).start()
        copy(0).wait()

    @pl.when((local == 1) & (block == 0))
    def arrived():
        copy(1).wait()

    rows, hidden_units = out_ref.shape[1], hidden_ref.shape[2]
    share = hidden_units // 32
    capacity = hidden_ref.shape[1] // 4
    x, y, z, own = place_ref[0], place_ref[1], place_ref[2], place_ref[3]
    row = lax.broadcasted_iota(jnp.int32, (rows, 1), 0) + block * rows
    row = row.astype(jnp.float32)
    tile = jnp.floor((row + 0.5) / share)
    rest = row - tile * share
    outer = jnp.floor((tile + 0.5) / 8.0)
    inner = jnp.floor((tile - outer * 8.0 + 0.5) / 2.0)
    last = tile - outer * 8.0 - inner * 2.0
    first = local == 0
    first_base = jnp.where(first, x, y).astype(jnp.float32)
    second_base = jnp.where(first, y, x).astype(jnp.float32)
    outer = outer + first_base
    outer = jnp.where(outer >= 4.0, outer - 4.0, outer)
    inner = inner + second_base
    inner = jnp.where(inner >= 4.0, inner - 4.0, inner)
    last = last + z.astype(jnp.float32)
    last = jnp.where(last >= 2.0, last - 2.0, last)
    outer_stride = jnp.where(first, 8, 1).astype(jnp.float32)
    inner_stride = jnp.where(first, 1, 8).astype(jnp.float32)
    source = (outer * outer_stride + inner * inner_stride + last * 4.0) * share + rest
    unit = lax.broadcasted_iota(jnp.int32, (rows, hidden_units), 1).astype(jnp.float32)
    pick = jnp.where(source == unit, 1.0, 0.0).astype(jnp.bfloat16)
    by_sender = jnp.concatenate(
        [
            hidden_ref[local, pl.ds(jnp.bitwise_xor(own, m) * capacity, capacity), :]
            for m in range(4)
        ],
        axis=0,
    )
    out_ref[0] = lax.dot_general(
        pick, by_sender, (((1,), (1,)), ((), ())), preferred_element_type=jnp.float32
    ).astype(jnp.bfloat16)


def prepare(place, hidden):
    local_count, slots, units = hidden.shape
    return pl.pallas_call(
        prepare_body,
        grid_spec=pltpu.PrefetchScalarGridSpec(
            num_scalar_prefetch=1,
            grid=(local_count, 4),
            in_specs=[pl.BlockSpec(memory_space=pltpu.HBM)],
            out_specs=pl.BlockSpec((1, units // 4, slots), lambda e, b, s: (e, b, 0)),
            scratch_shapes=[
                pltpu.VMEM(hidden.shape, hidden.dtype),
                pltpu.SemaphoreType.DMA((local_count,)),
            ],
        ),
        out_shape=jax.ShapeDtypeStruct((local_count, units, slots), jnp.bfloat16),
        compiler_params=pltpu.CompilerParams(vmem_limit_bytes=20 * 2**20),
        name="prepare",
    )(place, hidden)


def matmul_body(ring, hidden_ref, r0, r1, r2, r3, *out_refs):
    rhs = jnp.concatenate([r[0] for r in (r0, r1, r2, r3)], axis=0)
    product = jnp.dot(hidden_ref[0], rhs, preferred_element_type=jnp.float32)
    half = product.shape[0] // 2
    each = len(out_refs) // 2
    for local in range(2):
        outs = out_refs[each * local : each * (local + 1)]
        for j in range(4):

            @pl.when(pl.program_id(0) == 4 * local + j)
            def store(j=j, outs=outs):
                if ring and j == 2:
                    outs[3][...] = product[:half].astype(jnp.bfloat16)
                    outs[4][...] = product[half:].astype(jnp.bfloat16)
                else:
                    out = outs[2 if ring and j == 3 else j]
                    out[...] = product.astype(out.dtype)


def partials(hidden, near, far, offset, ring):
    capacity, part = far[0].shape[1:]
    rows, slots = hidden.shape[1] // 4, hidden.shape[2]
    wide = jax.ShapeDtypeStruct((rows, part), jnp.float32)
    if ring:
        shapes = [wide] * 3 + [jax.ShapeDtypeStruct((rows // 2, part), jnp.bfloat16)] * 2
    else:
        shapes = [wide] + [jax.ShapeDtypeStruct((rows, part), jnp.bfloat16)] * 3
    near_spec = pl.BlockSpec(
        (pl.Element(1), pl.Element(capacity), pl.Element(part)), lambda i: (i // 4, 0, offset)
    )
    far_spec = pl.BlockSpec((1, capacity, part), lambda i: (i // 4, 0, 0))
    outs = pl.pallas_call(
        functools.partial(matmul_body, ring),
        grid=(8,),
        in_specs=[
            pl.BlockSpec((1, rows, slots), lambda i: (i // 4, i % 4, 0)),
            near_spec,
            near_spec,
            far_spec,
            far_spec,
        ],
        out_specs=[pl.BlockSpec(s.shape, lambda i: (0, 0)) for s in shapes * 2],
        out_shape=shapes * 2,
        compiler_params=pltpu.CompilerParams(vmem_limit_bytes=NARROW),
    )(hidden, *near, *far)
    return outs[: len(shapes)], outs[len(shapes) :]


def to_half(total):
    return (total * 0.03125).astype(jnp.float16)


def from_half(block):
    return block.astype(jnp.float32) * 32.0


def ring_sum(own, ahead, behind, low, high, along):
    half = low.shape[0]
    high = send(high, along[1])
    low = send(low, along[3])
    ahead = jnp.concatenate([ahead[:half], ahead[half:] + high.astype(jnp.float32)])
    behind = jnp.concatenate([behind[:half] + low.astype(jnp.float32), behind[half:]])
    ahead, behind = to_half(ahead), to_half(behind)
    ahead = send(ahead, along[1])
    behind = send(behind, along[3])
    return own + from_half(ahead) + from_half(behind)


def quarters(total):
    rows = total.shape[0] // 4
    pieces = [total[j * rows : (j + 1) * rows] for j in range(4)]
    return pieces[0], [to_half(piece) for piece in pieces[1:]]


def direct_sum(own, sends, along):
    got = []
    for j, block in zip((1, 2, 3), sends):
        got.append(send(block, along[j]))
    for block in got:
        own = own + (from_half(block) if block.dtype == jnp.float16 else block.astype(jnp.float32))
    return own


def step(cotangent, route_ids, route_weights, hidden, master, first_moment, second_moment):
    groups = lax.axis_size("expert")
    capacity = hidden.shape[1] // groups
    dp = lax.axis_index("dp").astype(jnp.int32)
    own = lax.axis_index("expert").astype(jnp.int32)
    place = jnp.stack([dp // 8, dp % 4, dp // 4 % 2, own])
    ids, weights = route_ids.T, route_weights.T
    gradients, received = [], []
    start, turned = 0, None
    for group, widths in enumerate(GROUPS):
        if group == 1:
            place, _ = lax.optimization_barrier((place, received[0][1][0]))
            turned = prepare(place, hidden)
            own, turned = lax.optimization_barrier((own, turned))
        mine, partner, far, farther = dispatch(
            own[None], ids, weights, cotangent, widths, start, capacity
        )
        near = (mine, send(partner, TO_EXPERT[1]))
        offset = 0
        for index, width in enumerate(widths):
            one = send(far[index], TO_EXPERT[2])
            two = send(farther[index], TO_EXPERT[3])
            received.append((near, (mine, one, two), offset))
            offset += width
        start += sum(widths)
    totals = ([], [])
    for chunk, (near, (_, *far), offset) in enumerate(received):
        blocks = partials(turned, near, far, offset, RINGS[chunk])
        for local, along in enumerate((ALONG_X, ALONG_Y)):
            (own_block, *sends) = blocks[local]
            if RINGS[chunk]:
                total = ring_sum(own_block, *sends, along)
            else:
                total = direct_sum(own_block, sends, along)
            totals[local].append(total)
    for members in WAVES:
        halves = []
        for local, along in enumerate((ALONG_Y, ALONG_X)):
            total = jnp.concatenate([totals[local][c] for c in members], axis=1)
            own_block, sends = quarters(total)
            halves.append(direct_sum(own_block, sends, along))
        share = halves[0].shape[0] // 2
        away = jnp.stack([to_half(part[share:]) for part in halves])
        other = send(away, PAIR_Z)
        both = jnp.stack([part[:share] for part in halves]) + from_half(other)
        gradients.append(with_layout_constraint(both.transpose(1, 0, 2), ROW_MAJOR))
    summed = jnp.concatenate(gradients, axis=2)
    gradient = summed / jnp.sqrt(jnp.float32(groups * capacity))
    new_first = beta_one * first_moment + (1.0 - beta_one) * gradient
    new_second = beta_two * second_moment + (1.0 - beta_two) * gradient * gradient
    corrected_first = new_first / (1.0 - beta_one**step_count)
    corrected_second = new_second / (1.0 - beta_two**step_count)
    update = corrected_first / (jnp.sqrt(corrected_second) + epsilon) + decay_rate * master
    new_master = master - learning_rate * update
    return (new_master, new_first, new_second)


def solution(mesh):
    placed = (
        P(("dp", "expert"), None),
        P(("dp", "expert"), None),
        P(("dp", "expert"), None),
        P("expert", "dp", None),
        P("dp", "expert", None),
        P("dp", "expert", None),
        P("dp", "expert", None),
    )
    return jax.shard_map(
        step,
        mesh=mesh,
        in_specs=placed,
        out_specs=(P("dp", "expert", None), P("dp", "expert", None), P("dp", "expert", None)),
        check_vma=False,
    )
```

profile of v0, /device:TPU:102, one launch (start us, length us, event | category | flops | bytes accessed | tf_op | source)
XLA Modules:
  0.0 209.3 jit_solution(6493760105061646487)
XLA Ops:
  0.6 5.2 %shard_map.94 = (bf16[2,192,768]{2,1,0:T(8,128)(2,1)}, bf16[2,192,768]{2,1,0:T(8,128)(2,1)}, bf16[2,192,768]{2,1,0:T(8,128)(2,1)}, bf16[2,192,768]{2,1,0:T(8,128)(2,1)}) custom-call(s32[1]{0:T(128)} %bitcast.3.own_ref, s32[6,1024]{1,0:T(8,128)} %bitcast.23, f32[6,1024]{1,0:T(8,128)} %bitcast.25, bf16[1024,2048]{1,0:T(8,128)(2,1)} %cot_hbm.3), custom_call_target="tpu_custom_call" | custom-call | tf_op jit(solution)/shard_map/pallas_call | solution.py:114
  6.5 2.7 %collective-permute-start.2 = (bf16[2,192,768]{2,1,0:T(8,128)(2,1)}, bf16[2,192,768]{2,1,0:T(8,128)(2,1)S(1)}, u32[]{:S(2)}, u32[]{:S(2)}) collective-permute-start(bf16[2,192,768]{2,1,0:T(8,128)(2,1)} %get-tuple-element.49), channel_id=1, source_target_pairs={{0,3},{1,2},{16,19},{17,18},{2,1},{3,0},{18,17},{19,16},{4,7},{5,6... | collective-permute-start | bytes 1769480 | tf_op jit(solution)/shard_map/ppermute | solution.py:50
  9.3 2.2 %copy-done.1 = bf16[2,768,1408]{2,1,0:T(8,128)(2,1)S(1)} copy-done((bf16[2,768,1408]{2,1,0:T(8,128)(2,1)S(1)}, bf16[2,768,1408]{2,1,0:T(8,128)(2,1)}, u32[]{:S(2)}) %copy-start.1) | copy-done | bytes 4325400
  11.6 10.5 %prepare.1.hidden_ref = bf16[2,1408,768]{2,1,0:T(8,128)(2,1)S(1)} custom-call(s32[4]{0:T(128)S(1)} %pad_add_fusion.place_ref, bf16[2,768,1408]{2,1,0:T(8,128)(2,1)S(1)} %copy-done.1), custom_call_target="tpu_custom_call" | custom-call | tf_op jit(solution)/shard_map/prepare/pallas_call | solution.py:190
  23.9 11.5 %collective-permute-done.2.r3 = bf16[2,192,768]{2,1,0:T(8,128)(2,1)S(1)} collective-permute-done((bf16[2,192,768]{2,1,0:T(8,128)(2,1)}, bf16[2,192,768]{2,1,0:T(8,128)(2,1)S(1)}, u32[]{:S(2)}, u32[]{:S(2)}) %collective-permute-start.2) | collective-permute-done | bytes 589856 | tf_op jit(solution)/shard_map/ppermute | solution.py:50
  35.5 5.6 %shard_map.95 = (f32[352,768]{1,0:T(8,128)S(1)}, f32[352,768]{1,0:T(8,128)S(1)}, f32[352,768]{1,0:T(8,128)S(1)}, bf16[176,768]{1,0:T(8,128)(2,1)S(1)}, bf16[176,...) custom-call(bf16[2,1408,768]{2,1,0:T(8,128)(2,1)S(1)} %prepare.1.hid, ...), custom_call_target="tpu_custom_call" | custom-call | tf_op jit(solution)/shard_map/pallas_call | solution.py:239
  41.6 5.2 %shard_map.96 = (bf16[2,192,1280]{2,1,0:T(8,128)(2,1)S(1)}, bf16[2,192,1280]{2,1,0:T(8,128)(2,1)S(1)}, bf16[2,192,896]{2,1,0:T(8,128)(2,1)S(1)}, bf16[2,192,384]...) custom-call(s32[1]{0:T(128)} %bitcast.6.own_ref, s32[6,1024]{1,0:T(8,128)S(1)} %bitcast.24, ...), custom_call_target="tpu_custom_call" | custom-call | tf_op jit(solution)/shard_map/pallas_call | solution.py:114
  47.4 2.4 %collective-permute-start.30 = (bf16[2,192,384]{2,1,0:T(8,128)(2,1)S(1)}, bf16[2,192,384]{2,1,0:T(8,128)(2,1)S(1)}, u32[]{:S(2)}, u32[]{:S(2)}) collective-permute-start(bf16[2,192,384]{2,1,0:T(8,128)(2,1)S(1)} %get-tuple-element.76), channel_id=1, source_target_pairs={{0,3},{1,2},{16,19},{17,18},{2,1},{3,0},{18,17},{19,16},{4,7},{5,6... | collective-permute-start | bytes 884744 | tf_op jit(solution)/shard_map/ppermute | solution.py:50
  52.5 8.1 %collective-permute-done.5 = bf16[176,768]{1,0:T(8,128)(2,1)S(1)} collective-permute-done((bf16[176,768]{1,0:T(8,128)(2,1)S(1)}, bf16[176,768]{1,0:T(8,128)(2,1)S(1)}, u32[]{:S(2)}, u32[]{:S(2)}) %collective-permute-start.5) | collective-permute-done | bytes 270368 | tf_op jit(solution)/shard_map/ppermute | solution.py:50
  62.2 7.2 %collective-permute-done.17 = bf16[176,768]{1,0:T(8,128)(2,1)S(1)} collective-permute-done((bf16[176,768]{1,0:T(8,128)(2,1)S(1)}, bf16[176,768]{1,0:T(8,128)(2,1)S(1)}, u32[]{:S(2)}, u32[]{:S(2)}) %collective-permute-start.17) | collective-permute-done | bytes 270368 | tf_op jit(solution)/shard_map/ppermute | solution.py:50
  71.3 5.0 %collective-permute-done.19 = bf16[176,768]{1,0:T(8,128)(2,1)S(1)} collective-permute-done((bf16[176,768]{1,0:T(8,128)(2,1)S(1)}, bf16[176,768]{1,0:T(8,128)(2,1)S(1)}, u32[]{:S(2)}, u32[]{:S(2)}) %collective-permute-start.19) | collective-permute-done | bytes 270368 | tf_op jit(solution)/shard_map/ppermute | solution.py:50
  76.7 4.3 %shard_map.98 = (f32[352,384]{1,0:T(8,128)S(1)}, bf16[352,384]{1,0:T(8,128)(2,1)S(1)}, bf16[352,384]{1,0:T(8,128)(2,1)S(1)}, bf16[352,384]{1,0:T(8,128)(2,1)S(1)...) custom-call(bf16[2,1408,768]{2,1,0:T(8,128)(2,1)S(1)} %prepare.1.hid, ...), custom_call_target="tpu_custom_call" | custom-call | tf_op jit(solution)/shard_map/pallas_call | solution.py:239
  83.9 3.0 %collective-permute-start.20 = (f16[352,768]{1,0:T(8,128)(2,1)S(1)}, f16[352,768]{1,0:T(8,128)(2,1)S(1)}, u32[]{:S(2)}, u32[]{:S(2)}) collective-permute-start(f16[352,768]{1,0:T(8,128)(2,1)S(1)} %fusion.7), channel_id=1, source_target_pairs={{0,12},{1,13},{16,28},{17,29},{2,14},{3,15},{18,30},{19,31},{4,0},... | collective-permute-start | bytes 1622024 | tf_op jit(solution)/shard_map/ppermute | solution.py:50
  86.9 8.7 %collective-permute-done.9.r3 = bf16[2,192,896]{2,1,0:T(8,128)(2,1)S(1)} collective-permute-done((bf16[2,192,896]{2,1,0:T(8,128)(2,1)S(1)}, bf16[2,192,896]{2,1,0:T(8,128)(2,1)S(1)}, u32[]{:S(2)}, u32[]{:S(2)}) %collective-permute-start.9) | collective-permute-done | bytes 688160 | tf_op jit(solution)/shard_map/ppermute | solution.py:50
  95.8 7.0 %shard_map.97 = (f32[352,896]{1,0:T(8,128)S(1)}, f32[352,896]{1,0:T(8,128)S(1)}, f32[352,896]{1,0:T(8,128)S(1)}, bf16[176,896]{1,0:T(8,128)(2,1)S(1)}, bf16[176,...) custom-call(bf16[2,1408,768]{2,1,0:T(8,128)(2,1)S(1)} %prepare.1.hid, ...), custom_call_target="tpu_custom_call" | custom-call | tf_op jit(solution)/shard_map/pallas_call | solution.py:239
  104.4 2.9 %collective-permute-start.38 = (bf16[352,384]{1,0:T(8,128)(2,1)S(1)}, bf16[352,384]{1,0:T(8,128)(2,1)S(1)}, u32[]{:S(2)}, u32[]{:S(2)}) collective-permute-start(bf16[352,384]{1,0:T(8,128)(2,1)S(1)} %get-tuple-element.83), channel_id=1, source_target_pairs={{0,8},{1,9},{16,24},{17,25},{2,10},{3,11},{18,26},{19,27},{4,12},{... | collective-permute-start | bytes 811016 | tf_op jit(solution)/shard_map/ppermute | solution.py:50
  107.3 2.3 %collective-permute-start.39 = (bf16[352,384]{1,0:T(8,128)(2,1)S(1)}, bf16[352,384]{1,0:T(8,128)(2,1)S(1)}, u32[]{:S(2)}, u32[]{:S(2)}) collective-permute-start(bf16[352,384]{1,0:T(8,128)(2,1)S(1)} %get-tuple-element.84), channel_id=1, source_target_pairs={{0,12},{1,13},{16,28},{17,29},{2,14},{3,15},{18,30},{19,31},{4,0},... | collective-permute-start | bytes 811016 | tf_op jit(solution)/shard_map/ppermute | solution.py:50
  109.7 7.1 %collective-permute-done.37 = bf16[352,384]{1,0:T(8,128)(2,1)S(1)} collective-permute-done((bf16[352,384]{1,0:T(8,128)(2,1)S(1)}, bf16[352,384]{1,0:T(8,128)(2,1)S(1)}, u32[]{:S(2)}, u32[]{:S(2)}) %collective-permute-start.37) | collective-permute-done | bytes 270368 | tf_op jit(solution)/shard_map/ppermute | solution.py:50
  117.2 6.7 %collective-permute-done.38 = bf16[352,384]{1,0:T(8,128)(2,1)S(1)} collective-permute-done((bf16[352,384]{1,0:T(8,128)(2,1)S(1)}, bf16[352,384]{1,0:T(8,128)(2,1)S(1)}, u32[]{:S(2)}, u32[]{:S(2)}) %collective-permute-start.38) | collective-permute-done | bytes 270368 | tf_op jit(solution)/shard_map/ppermute | solution.py:50
  127.6 5.9 %collective-permute-done.12 = bf16[176,896]{1,0:T(8,128)(2,1)S(1)} collective-permute-done((bf16[176,896]{1,0:T(8,128)(2,1)S(1)}, bf16[176,896]{1,0:T(8,128)(2,1)S(1)}, u32[]{:S(2)}, u32[]{:S(2)}) %collective-permute-start.12) | collective-permute-done | bytes 315424 | tf_op jit(solution)/shard_map/ppermute | solution.py:50
  133.7 3.3 %collective-permute-start.36 = (f16[88,384]{1,0:T(8,128)(2,1)S(1)}, f16[88,384]{1,0:T(8,128)(2,1)S(1)}, u32[]{:S(2)}, u32[]{:S(2)}) collective-permute-start(f16[88,384]{1,0:T(8,128)(2,1)S(1)} %get-tuple-element.115), channel_id=1, source_target_pairs={{0,12},{1,13},{16,28},{17,29},{2,14},{3,15},{18,30},{19,31},{4,0},... | collective-permute-start | bytes 202760 | tf_op jit(solution)/shard_map/ppermute | solution.py:50
  141.1 2.3 %collective-permute-done.35 = f16[88,384]{1,0:T(8,128)(2,1)S(1)} collective-permute-done((f16[88,384]{1,0:T(8,128)(2,1)S(1)}, f16[88,384]{1,0:T(8,128)(2,1)S(1)}, u32[]{:S(2)}, u32[]{:S(2)}) %collective-permute-start.35) | collective-permute-done | bytes 67616 | tf_op jit(solution)/shard_map/ppermute | solution.py:50
  146.9 3.0 %collective-permute-done.41 = f16[88,384]{1,0:T(8,128)(2,1)S(1)} collective-permute-done((f16[88,384]{1,0:T(8,128)(2,1)S(1)}, f16[88,384]{1,0:T(8,128)(2,1)S(1)}, u32[]{:S(2)}, u32[]{:S(2)}) %collective-permute-start.41) | collective-permute-done | bytes 67616 | tf_op jit(solution)/shard_map/ppermute | solution.py:50
  150.1 3.3 %collective-permute-start.11 = (f16[352,896]{1,0:T(8,128)(2,1)S(1)}, f16[352,896]{1,0:T(8,128)(2,1)S(1)}, u32[]{:S(2)}, u32[]{:S(2)}) collective-permute-start(f16[352,896]{1,0:T(8,128)(2,1)S(1)} %fusion), channel_id=1, source_target_pairs={{0,32},{1,33},{16,48},{17,49},{2,34},{3,35},{18,50},{19,51},{4,36}... | collective-permute-start | bytes 1892360 | tf_op jit(solution)/shard_map/ppermute | solution.py:50
  153.9 6.8 %collective-permute-done.6 = f16[352,768]{1,0:T(8,128)(2,1)S(1)} collective-permute-done((f16[352,768]{1,0:T(8,128)(2,1)S(1)}, f16[352,768]{1,0:T(8,128)(2,1)S(1)}, u32[]{:S(2)}, u32[]{:S(2)}) %collective-permute-start.6) | collective-permute-done | bytes 540704 | tf_op jit(solution)/shard_map/ppermute | solution.py:50
  161.9 9.3 %collective-permute-done.13 = f16[352,896]{1,0:T(8,128)(2,1)S(1)} collective-permute-done((f16[352,896]{1,0:T(8,128)(2,1)S(1)}, f16[352,896]{1,0:T(8,128)(2,1)S(1)}, u32[]{:S(2)}, u32[]{:S(2)}) %collective-permute-start.13) | collective-permute-done | bytes 630816 | tf_op jit(solution)/shard_map/ppermute | solution.py:50
  171.8 3.2 %collective-permute-start.16 = (f16[88,1664]{1,0:T(8,128)(2,1)S(1)}, f16[88,1664]{1,0:T(8,128)(2,1)S(1)}, u32[]{:S(2)}, u32[]{:S(2)}) collective-permute-start(f16[88,1664]{1,0:T(8,128)(2,1)S(1)} %get-tuple-element.89), channel_id=1, source_target_pairs={{0,12},{1,13},{16,28},{17,29},{2,14},{3,15},{18,30},{19,31},{4,0},... | collective-permute-start | bytes 878600 | tf_op jit(solution)/shard_map/ppermute | solution.py:50
  175.5 2.2 %collective-permute-start.25 = (f16[88,1664]{1,0:T(8,128)(2,1)S(1)}, f16[88,1664]{1,0:T(8,128)(2,1)S(1)}, u32[]{:S(2)}, u32[]{:S(2)}) collective-permute-start(f16[88,1664]{1,0:T(8,128)(2,1)S(1)} %get-tuple-element.91), channel_id=1, source_target_pairs={{0,32},{1,33},{16,48},{17,49},{2,34},{3,35},{18,50},{19,51},{4,36}... | collective-permute-start | bytes 878600 | tf_op jit(solution)/shard_map/ppermute | solution.py:50
  177.6 7.9 %collective-permute-done.14 = f16[88,1664]{1,0:T(8,128)(2,1)S(1)} collective-permute-done((f16[88,1664]{1,0:T(8,128)(2,1)S(1)}, f16[88,1664]{1,0:T(8,128)(2,1)S(1)}, u32[]{:S(2)}, u32[]{:S(2)}) %collective-permute-start.14) | collective-permute-done | bytes 292896 | tf_op jit(solution)/shard_map/ppermute | solution.py:50
  188.3 8.3 %collective-permute-done.27 = f16[88,1664]{1,0:T(8,128)(2,1)S(1)} collective-permute-done((f16[88,1664]{1,0:T(8,128)(2,1)S(1)}, f16[88,1664]{1,0:T(8,128)(2,1)S(1)}, u32[]{:S(2)}, u32[]{:S(2)}) %collective-permute-start.27) | collective-permute-done | bytes 292896 | tf_op jit(solution)/shard_map/ppermute | solution.py:50
  199.0 5.8 %collective-permute-done.28 = f16[2,44,1664]{2,0,1:T(2,128)(2,1)S(1)} collective-permute-done((f16[2,44,1664]{2,0,1:T(2,128)(2,1)S(1)}, f16[2,44,1664]{2,0,1:T(2,128)(2,1)S(1)}, u32[]{:S(2)}, u32[]{:S(2)}) %collective-permute-start.28) | collective-permute-done | bytes 292896 | tf_op jit(solution)/shard_map/ppermute | solution.py:50
  205.5 3.8 %multiply_subtract_fusion = (f32[44,2,2048]{2,1,0:T(2,128)}, f32[44,2,2048]{2,1,0:T(2,128)}, f32[44,2,2048]{2,1,0:T(2,128)}) fusion(f32[44,2,2048]{2,1,0:T(2,128)S(1)} %copy-done.5, f32[44,2,384]{2,1,0:T(2,128)S(1)} %fusion.47, f32[44,2,1664]{2,1,0:T(2,128)S(1)} %fusion.32, f32[44,2,2048]{2,1,0:T(2,128)S(1)} %copy-done.6, f32[44,2,2048]{2,1,0:T(2,128)S(1)} %copy-done.7), kind=kLoop, calls=%fused_computation.33 | loop fusion | flops 3063808 | bytes 5046272 | tf_op jit(solution)/shard_map/sub | solution.py:344
  (126 shorter events, 35.4 us)
Async XLA Ops:
  5.8 16.3 %collective-permute-start = (bf16[2,192,768]{2,1,0:T(8,128)(2,1)}, bf16[2,192,768]{2,1,0:T(8,128)(2,1)S(1)}, u32[]{:S(2)}, u32[]{:S(2)}) collective-permute-start(bf16[2,192,768]{2,1,0:T(8,128)(2,1)} %get-tuple-element.47), channel_id=1, source_target_pairs={{0,1},{1,0},{16,17},{17,16},{2,3},{3,2},{18,19},{19,18},{4,5},{5,4... | collective-permute-start | bytes 1769480 | tf_op jit(solution)/shard_map/ppermute | solution.py:50
  5.9 18.0 %collective-permute-start.1 = (bf16[2,192,768]{2,1,0:T(8,128)(2,1)}, bf16[2,192,768]{2,1,0:T(8,128)(2,1)S(1)}, u32[]{:S(2)}, u32[]{:S(2)}) collective-permute-start(bf16[2,192,768]{2,1,0:T(8,128)(2,1)} %get-tuple-element.48), channel_id=1, source_target_pairs={{0,2},{1,3},{16,18},{17,19},{2,0},{3,1},{18,16},{19,17},{4,6},{5,7... | collective-permute-start | bytes 1769480 | tf_op jit(solution)/shard_map/ppermute | solution.py:50
  6.5 28.9 %collective-permute-start.2 = (bf16[2,192,768]{2,1,0:T(8,128)(2,1)}, bf16[2,192,768]{2,1,0:T(8,128)(2,1)S(1)}, u32[]{:S(2)}, u32[]{:S(2)}) collective-permute-start(bf16[2,192,768]{2,1,0:T(8,128)(2,1)} %get-tuple-element.49), channel_id=1, source_target_pairs={{0,3},{1,2},{16,19},{17,18},{2,1},{3,0},{18,17},{19,16},{4,7},{5,6... | collective-permute-start | bytes 1769480 | tf_op jit(solution)/shard_map/ppermute | solution.py:50
  41.0 9.8 %collective-permute-start.3 = (bf16[176,768]{1,0:T(8,128)(2,1)S(1)}, bf16[176,768]{1,0:T(8,128)(2,1)S(1)}, u32[]{:S(2)}, u32[]{:S(2)}) collective-permute-start(bf16[176,768]{1,0:T(8,128)(2,1)S(1)} %get-tuple-element.52), channel_id=1, source_target_pairs={{0,32},{1,33},{16,48},{17,49},{2,34},{3,35},{18,50},{19,51},{4,36}... | collective-permute-start | bytes 811016 | tf_op jit(solution)/shard_map/ppermute | solution.py:50
  46.8 29.8 %collective-permute-start.29 = (bf16[2,192,384]{2,1,0:T(8,128)(2,1)S(1)}, bf16[2,192,384]{2,1,0:T(8,128)(2,1)S(1)}, u32[]{:S(2)}, u32[]{:S(2)}) collective-permute-start(bf16[2,192,384]{2,1,0:T(8,128)(2,1)S(1)} %get-tuple-element.75), channel_id=1, source_target_pairs={{0,2},{1,3},{16,18},{17,19},{2,0},{3,1},{18,16},{19,17},{4,6},{5,7... | collective-permute-start | bytes 884744 | tf_op jit(solution)/shard_map/ppermute | solution.py:50
  47.4 29.2 %collective-permute-start.30 = (bf16[2,192,384]{2,1,0:T(8,128)(2,1)S(1)}, bf16[2,192,384]{2,1,0:T(8,128)(2,1)S(1)}, u32[]{:S(2)}, u32[]{:S(2)}) collective-permute-start(bf16[2,192,384]{2,1,0:T(8,128)(2,1)S(1)} %get-tuple-element.76), channel_id=1, source_target_pairs={{0,3},{1,2},{16,19},{17,18},{2,1},{3,0},{18,17},{19,16},{4,7},{5,6... | collective-permute-start | bytes 884744 | tf_op jit(solution)/shard_map/ppermute | solution.py:50
  49.9 34.0 %collective-permute-start.8 = (bf16[2,192,896]{2,1,0:T(8,128)(2,1)S(1)}, bf16[2,192,896]{2,1,0:T(8,128)(2,1)S(1)}, u32[]{:S(2)}, u32[]{:S(2)}) collective-permute-start(bf16[2,192,896]{2,1,0:T(8,128)(2,1)S(1)} %get-tuple-element.58), channel_id=1, source_target_pairs={{0,2},{1,3},{16,18},{17,19},{2,0},{3,1},{18,16},{19,17},{4,6},{5,7... | collective-permute-start | bytes 2064392 | tf_op jit(solution)/shard_map/ppermute | solution.py:50
  50.4 26.2 %collective-permute-start.7 = (bf16[2,192,1280]{2,1,0:T(8,128)(2,1)S(1)}, bf16[2,192,1280]{2,1,0:T(8,128)(2,1)S(1)}, u32[]{:S(2)}, u32[]{:S(2)}) collective-permute-start(bf16[2,192,1280]{2,1,0:T(8,128)(2,1)S(1)} %get-tuple-element.57), channel_id=1, source_target_pairs={{0,1},{1,0},{16,17},{17,16},{2,3},{3,2},{18,19},{19,18},{4,5},{5,4... | collective-permute-start | bytes 2949128 | tf_op jit(solution)/shard_map/ppermute | solution.py:50
  50.8 9.7 %collective-permute-start.5 = (bf16[176,768]{1,0:T(8,128)(2,1)S(1)}, bf16[176,768]{1,0:T(8,128)(2,1)S(1)}, u32[]{:S(2)}, u32[]{:S(2)}) collective-permute-start(bf16[176,768]{1,0:T(8,128)(2,1)S(1)} %get-tuple-element.54), channel_id=1, source_target_pairs={{0,96},{1,97},{16,112},{17,113},{2,98},{3,99},{18,114},{19,115},{4... | collective-permute-start | bytes 811016 | tf_op jit(solution)/shard_map/ppermute | solution.py:50
  76.3 19.2 %collective-permute-start.9 = (bf16[2,192,896]{2,1,0:T(8,128)(2,1)S(1)}, bf16[2,192,896]{2,1,0:T(8,128)(2,1)S(1)}, u32[]{:S(2)}, u32[]{:S(2)}) collective-permute-start(bf16[2,192,896]{2,1,0:T(8,128)(2,1)S(1)} %get-tuple-element.59), channel_id=1, source_target_pairs={{0,3},{1,2},{16,19},{17,18},{2,1},{3,0},{18,17},{19,16},{4,7},{5,6... | collective-permute-start | bytes 2064392 | tf_op jit(solution)/shard_map/ppermute | solution.py:50
  81.0 21.8 %collective-permute-start.31 = (bf16[352,384]{1,0:T(8,128)(2,1)S(1)}, bf16[352,384]{1,0:T(8,128)(2,1)S(1)}, u32[]{:S(2)}, u32[]{:S(2)}) collective-permute-start(bf16[352,384]{1,0:T(8,128)(2,1)S(1)} %get-tuple-element.78), channel_id=1, source_target_pairs={{0,32},{1,33},{16,48},{17,49},{2,34},{3,35},{18,50},{19,51},{4,36}... | collective-permute-start | bytes 811016 | tf_op jit(solution)/shard_map/ppermute | solution.py:50
  81.5 23.0 %collective-permute-start.32 = (bf16[352,384]{1,0:T(8,128)(2,1)S(1)}, bf16[352,384]{1,0:T(8,128)(2,1)S(1)}, u32[]{:S(2)}, u32[]{:S(2)}) collective-permute-start(bf16[352,384]{1,0:T(8,128)(2,1)S(1)} %get-tuple-element.79), channel_id=1, source_target_pairs={{0,64},{1,65},{16,80},{17,81},{2,66},{3,67},{18,82},{19,83},{4,68}... | collective-permute-start | bytes 811016 | tf_op jit(solution)/shard_map/ppermute | solution.py:50
  83.3 24.0 %collective-permute-start.33 = (bf16[352,384]{1,0:T(8,128)(2,1)S(1)}, bf16[352,384]{1,0:T(8,128)(2,1)S(1)}, u32[]{:S(2)}, u32[]{:S(2)}) collective-permute-start(bf16[352,384]{1,0:T(8,128)(2,1)S(1)} %get-tuple-element.80), channel_id=1, source_target_pairs={{0,96},{1,97},{16,112},{17,113},{2,98},{3,99},{18,114},{19,115},{4... | collective-permute-start | bytes 811016 | tf_op jit(solution)/shard_map/ppermute | solution.py:50
  83.9 66.2 %collective-permute-start.20 = (f16[352,768]{1,0:T(8,128)(2,1)S(1)}, f16[352,768]{1,0:T(8,128)(2,1)S(1)}, u32[]{:S(2)}, u32[]{:S(2)}) collective-permute-start(f16[352,768]{1,0:T(8,128)(2,1)S(1)} %fusion.7), channel_id=1, source_target_pairs={{0,12},{1,13},{16,28},{17,29},{2,14},{3,15},{18,30},{19,31},{4,0},... | collective-permute-start | bytes 1622024 | tf_op jit(solution)/shard_map/ppermute | solution.py:50
  95.5 58.0 %collective-permute-start.18 = (f16[352,768]{1,0:T(8,128)(2,1)S(1)}, f16[352,768]{1,0:T(8,128)(2,1)S(1)}, u32[]{:S(2)}, u32[]{:S(2)}) collective-permute-start(f16[352,768]{1,0:T(8,128)(2,1)S(1)} %fusion.6), channel_id=1, source_target_pairs={{0,4},{1,5},{16,20},{17,21},{2,6},{3,7},{18,22},{19,23},{4,8},{5,9... | collective-permute-start | bytes 1622024 | tf_op jit(solution)/shard_map/ppermute | solution.py:50
  102.8 14.0 %collective-permute-start.37 = (bf16[352,384]{1,0:T(8,128)(2,1)S(1)}, bf16[352,384]{1,0:T(8,128)(2,1)S(1)}, u32[]{:S(2)}, u32[]{:S(2)}) collective-permute-start(bf16[352,384]{1,0:T(8,128)(2,1)S(1)} %get-tuple-element.82), channel_id=1, source_target_pairs={{0,4},{1,5},{16,20},{17,21},{2,6},{3,7},{18,22},{19,23},{4,8},{5,9... | collective-permute-start | bytes 811016 | tf_op jit(solution)/shard_map/ppermute | solution.py:50
  104.4 19.5 %collective-permute-start.38 = (bf16[352,384]{1,0:T(8,128)(2,1)S(1)}, bf16[352,384]{1,0:T(8,128)(2,1)S(1)}, u32[]{:S(2)}, u32[]{:S(2)}) collective-permute-start(bf16[352,384]{1,0:T(8,128)(2,1)S(1)} %get-tuple-element.83), channel_id=1, source_target_pairs={{0,8},{1,9},{16,24},{17,25},{2,10},{3,11},{18,26},{19,27},{4,12},{... | collective-permute-start | bytes 811016 | tf_op jit(solution)/shard_map/ppermute | solution.py:50
  107.3 16.7 %collective-permute-start.39 = (bf16[352,384]{1,0:T(8,128)(2,1)S(1)}, bf16[352,384]{1,0:T(8,128)(2,1)S(1)}, u32[]{:S(2)}, u32[]{:S(2)}) collective-permute-start(bf16[352,384]{1,0:T(8,128)(2,1)S(1)} %get-tuple-element.84), channel_id=1, source_target_pairs={{0,12},{1,13},{16,28},{17,29},{2,14},{3,15},{18,30},{19,31},{4,0},... | collective-permute-start | bytes 811016 | tf_op jit(solution)/shard_map/ppermute | solution.py:50
  125.4 12.0 %collective-permute-start.23 = (bf16[176,896]{1,0:T(8,128)(2,1)S(1)}, bf16[176,896]{1,0:T(8,128)(2,1)S(1)}, u32[]{:S(2)}, u32[]{:S(2)}) collective-permute-start(bf16[176,896]{1,0:T(8,128)(2,1)S(1)} %get-tuple-element.74), channel_id=1, source_target_pairs={{0,12},{1,13},{16,28},{17,29},{2,14},{3,15},{18,30},{19,31},{4,0},... | collective-permute-start | bytes 946184 | tf_op jit(solution)/shard_map/ppermute | solution.py:50
  143.5 17.2 %collective-permute-start.6 = (f16[352,768]{1,0:T(8,128)(2,1)S(1)}, f16[352,768]{1,0:T(8,128)(2,1)S(1)}, u32[]{:S(2)}, u32[]{:S(2)}) collective-permute-start(f16[352,768]{1,0:T(8,128)(2,1)S(1)} %fusion.5), channel_id=1, source_target_pairs={{0,96},{1,97},{16,112},{17,113},{2,98},{3,99},{18,114},{19,115},{4... | collective-permute-start | bytes 1622024 | tf_op jit(solution)/shard_map/ppermute | solution.py:50
  146.3 15.1 %collective-permute-start.4 = (f16[352,768]{1,0:T(8,128)(2,1)S(1)}, f16[352,768]{1,0:T(8,128)(2,1)S(1)}, u32[]{:S(2)}, u32[]{:S(2)}) collective-permute-start(f16[352,768]{1,0:T(8,128)(2,1)S(1)} %fusion.4), channel_id=1, source_target_pairs={{0,32},{1,33},{16,48},{17,49},{2,34},{3,35},{18,50},{19,51},{4,36}... | collective-permute-start | bytes 1622024 | tf_op jit(solution)/shard_map/ppermute | solution.py:50
  149.9 21.4 %collective-permute-start.13 = (f16[352,896]{1,0:T(8,128)(2,1)S(1)}, f16[352,896]{1,0:T(8,128)(2,1)S(1)}, u32[]{:S(2)}, u32[]{:S(2)}) collective-permute-start(f16[352,896]{1,0:T(8,128)(2,1)S(1)} %fusion.1), channel_id=1, source_target_pairs={{0,96},{1,97},{16,112},{17,113},{2,98},{3,99},{18,114},{19,115},{4... | collective-permute-start | bytes 1892360 | tf_op jit(solution)/shard_map/ppermute | solution.py:50
  150.1 21.2 %collective-permute-start.11 = (f16[352,896]{1,0:T(8,128)(2,1)S(1)}, f16[352,896]{1,0:T(8,128)(2,1)S(1)}, u32[]{:S(2)}, u32[]{:S(2)}) collective-permute-start(f16[352,896]{1,0:T(8,128)(2,1)S(1)} %fusion), channel_id=1, source_target_pairs={{0,32},{1,33},{16,48},{17,49},{2,34},{3,35},{18,50},{19,51},{4,36}... | collective-permute-start | bytes 1892360 | tf_op jit(solution)/shard_map/ppermute | solution.py:50
  153.6 21.4 %collective-permute-start.24 = (f16[352,896]{1,0:T(8,128)(2,1)S(1)}, f16[352,896]{1,0:T(8,128)(2,1)S(1)}, u32[]{:S(2)}, u32[]{:S(2)}) collective-permute-start(f16[352,896]{1,0:T(8,128)(2,1)S(1)} %fusion.3), channel_id=1, source_target_pairs={{0,12},{1,13},{16,28},{17,29},{2,14},{3,15},{18,30},{19,31},{4,0},... | collective-permute-start | bytes 1892360 | tf_op jit(solution)/shard_map/ppermute | solution.py:50
  160.7 14.3 %collective-permute-start.22 = (f16[352,896]{1,0:T(8,128)(2,1)S(1)}, f16[352,896]{1,0:T(8,128)(2,1)S(1)}, u32[]{:S(2)}, u32[]{:S(2)}) collective-permute-start(f16[352,896]{1,0:T(8,128)(2,1)S(1)} %fusion.2), channel_id=1, source_target_pairs={{0,4},{1,5},{16,20},{17,21},{2,6},{3,7},{18,22},{19,23},{4,8},{5,9... | collective-permute-start | bytes 1892360 | tf_op jit(solution)/shard_map/ppermute | solution.py:50
  161.5 36.8 %collective-permute-start.43 = (f16[2,44,384]{2,0,1:T(2,128)(2,1)S(1)}, f16[2,44,384]{2,0,1:T(2,128)(2,1)S(1)}, u32[]{:S(2)}, u32[]{:S(2)}) collective-permute-start(f16[2,44,384]{2,0,1:T(2,128)(2,1)S(1)} %pad_maximum_fusion.4), channel_id=1, source_target_pairs={{0,16},{1,17},{16,0},{17,1},{2,18},{3,19},{18,2},{19,3},{4,20},{5,... | collective-permute-start | bytes 202760 | tf_op jit(solution)/shard_map/ppermute | solution.py:50
  171.7 13.8 %collective-permute-start.14 = (f16[88,1664]{1,0:T(8,128)(2,1)S(1)}, f16[88,1664]{1,0:T(8,128)(2,1)S(1)}, u32[]{:S(2)}, u32[]{:S(2)}) collective-permute-start(f16[88,1664]{1,0:T(8,128)(2,1)S(1)} %get-tuple-element.88), channel_id=1, source_target_pairs={{0,4},{1,5},{16,20},{17,21},{2,6},{3,7},{18,22},{19,23},{4,8},{5,9... | collective-permute-start | bytes 878600 | tf_op jit(solution)/shard_map/ppermute | solution.py:50
  171.8 13.8 %collective-permute-start.16 = (f16[88,1664]{1,0:T(8,128)(2,1)S(1)}, f16[88,1664]{1,0:T(8,128)(2,1)S(1)}, u32[]{:S(2)}, u32[]{:S(2)}) collective-permute-start(f16[88,1664]{1,0:T(8,128)(2,1)S(1)} %get-tuple-element.89), channel_id=1, source_target_pairs={{0,12},{1,13},{16,28},{17,29},{2,14},{3,15},{18,30},{19,31},{4,0},... | collective-permute-start | bytes 878600 | tf_op jit(solution)/shard_map/ppermute | solution.py:50
  175.0 12.7 %collective-permute-start.15 = (f16[88,1664]{1,0:T(8,128)(2,1)S(1)}, f16[88,1664]{1,0:T(8,128)(2,1)S(1)}, u32[]{:S(2)}, u32[]{:S(2)}) collective-permute-start(f16[88,1664]{1,0:T(8,128)(2,1)S(1)} %get-tuple-element.90), channel_id=1, source_target_pairs={{0,8},{1,9},{16,24},{17,25},{2,10},{3,11},{18,26},{19,27},{4,12},{... | collective-permute-start | bytes 878600 | tf_op jit(solution)/shard_map/ppermute | solution.py:50
  175.5 12.9 %collective-permute-start.25 = (f16[88,1664]{1,0:T(8,128)(2,1)S(1)}, f16[88,1664]{1,0:T(8,128)(2,1)S(1)}, u32[]{:S(2)}, u32[]{:S(2)}) collective-permute-start(f16[88,1664]{1,0:T(8,128)(2,1)S(1)} %get-tuple-element.91), channel_id=1, source_target_pairs={{0,32},{1,33},{16,48},{17,49},{2,34},{3,35},{18,50},{19,51},{4,36}... | collective-permute-start | bytes 878600 | tf_op jit(solution)/shard_map/ppermute | solution.py:50
  185.5 11.1 %collective-permute-start.27 = (f16[88,1664]{1,0:T(8,128)(2,1)S(1)}, f16[88,1664]{1,0:T(8,128)(2,1)S(1)}, u32[]{:S(2)}, u32[]{:S(2)}) collective-permute-start(f16[88,1664]{1,0:T(8,128)(2,1)S(1)} %get-tuple-element.92), channel_id=1, source_target_pairs={{0,96},{1,97},{16,112},{17,113},{2,98},{3,99},{18,114},{19,115},{4... | collective-permute-start | bytes 878600 | tf_op jit(solution)/shard_map/ppermute | solution.py:50
  185.6 11.0 %collective-permute-start.26 = (f16[88,1664]{1,0:T(8,128)(2,1)S(1)}, f16[88,1664]{1,0:T(8,128)(2,1)S(1)}, u32[]{:S(2)}, u32[]{:S(2)}) collective-permute-start(f16[88,1664]{1,0:T(8,128)(2,1)S(1)} %get-tuple-element.93), channel_id=1, source_target_pairs={{0,64},{1,65},{16,80},{17,81},{2,66},{3,67},{18,82},{19,83},{4,68}... | collective-permute-start | bytes 878600 | tf_op jit(solution)/shard_map/ppermute | solution.py:50
  (20 other events, 177.9 us)
where the time goes:
time: 210 us; the launch traced here: 209 us
  waiting for transfers between devices  110 us (52%)
  starting transfers between devices  46.6 us (22%)
  Pallas kernels  37.8 us (18%)
  other arithmetic  9.63 us (5%)
  local copies, waits for them, and re-layouts  3.75 us (2%)
    ppermute x44, waiting for transfers between devices, send(): return lax.ppermute(array, AXES, pairs)  110 us
    ppermute x44, starting transfers between devices, send(): return lax.ppermute(array, AXES, pairs)  46.6 us
    pallas_call x3, Pallas kernels, partials(): pl.pallas_call(functools.partial(matmul_body, ring), grid=(8,), in_specs=...  16.9 us
    pallas_call x1, Pallas kernels, prepare(): pl.pallas_call(prepare_body, grid_spec=pltpu.PrefetchScalarGridSpec(num_s...  10.5 us
    pallas_call x2, Pallas kernels, dispatch(): pl.pallas_call(functools.partial(dispatch_body, start), grid_spec=pltpu.P...  10.4 us
  transfers between devices with their start and end apart: 44, of which 20 were waited for; matrix products, arithmetic and copies ran while one was open for 3% of the time, Pallas kernels for 13%

commit v1 on v0

--- a/solution.py
+++ b/solution.py
@@ -16,9 +16,9 @@
 decay_rate = 0.1
 step_count = 4.0
 
-GROUPS = ((768,), (896, 384))
+GROUPS = ((768,), (768, 512))
 WAVES = ((0, 1), (2,))
-RINGS = (True, True, False)
+RINGS = (False, True, False)
 ROW_MAJOR = Layout(major_to_minor=(0, 1, 2))
 WIDE, NARROW = 60 * 1024 * 2**10, 24 * 2**20
 AXES = ("dp", "expert")
@@ -50,11 +50,11 @@
     return lax.ppermute(array, AXES, pairs)
 
 
-def dispatch_body(start, own_ref, ids_hbm, weights_hbm, cot_hbm, *refs):
+def dispatch_body(start, near, own_ref, ids_hbm, weights_hbm, cot_hbm, *refs):
     out_refs, (ids_ref, weights_ref, cot_ref, sems) = refs[:-4], refs[-4:]
     capacity = out_refs[0].shape[1]
     tokens, part = cot_ref.shape
-    columns = cot_hbm.at[:, pl.ds(start, part)]
+    columns = cot_hbm.at[:, pl.ds(0, part)]
     pairs = ((ids_hbm, ids_ref), (weights_hbm, weights_ref), (columns, cot_ref))
     copies = [pltpu.make_async_copy(a, b, sems.at[n]) for n, (a, b) in enumerate(pairs)]
     for copy in copies:
@@ -77,22 +77,23 @@
     ahead = ahead.astype(jnp.float32).astype(jnp.bfloat16)
     offset = jnp.zeros((8, 1), jnp.float32)
     ranks = []
-    for start in range(0, tokens, 128):
-        tile = taken[:, start : start + 128]
+    for first in range(0, tokens, 128):
+        tile = taken[:, first : first + 128]
         inside = jnp.dot(tile.astype(jnp.bfloat16), ahead, preferred_element_type=jnp.float32)
         ranks.append(jnp.where(tile > 0.0, inside + offset, -1.0))
         offset = offset + jnp.sum(tile, axis=1, keepdims=True)
     rank = jnp.concatenate(ranks, axis=1).astype(jnp.int32)
     slot = lax.broadcasted_iota(jnp.int32, (capacity, tokens), 0)
-    far = (len(out_refs) - 2) // 2
+    far_refs = out_refs[2:] if near else out_refs
+    far = len(far_refs) // 2
     copies[2].wait()
-    for m in (2, 3, 1, 0):
+    for m in (2, 3, 1, 0) if near else (2, 3):
         for local in range(2):
             k = 2 * m + local
             mask = rank[k : k + 1, :] == slot
             picked = jnp.dot(
                 jnp.where(mask, 1.0, 0.0).astype(jnp.bfloat16),
-                cot_ref[...],
+                cot_ref[...] if m < 2 else cot_ref[:, start:],
                 preferred_element_type=jnp.float32,
             )
             weight = jnp.sum(jnp.where(mask, weight_rows[k], 0.0), axis=1, keepdims=True)
@@ -101,18 +102,18 @@
                 out_refs[m][local] = rows
             else:
                 at = 0
-                for out in out_refs[2 + far * (m - 2) : 2 + far * (m - 1)]:
+                for out in far_refs[far * (m - 2) : far * (m - 1)]:
                     out[local] = rows[:, at : at + out.shape[2]]
                     at += out.shape[2]
 
 
-def dispatch(own, ids, weights, cotangent, widths, start, capacity):
-    tokens = cotangent.shape[0]
-    part = sum(widths)
+def dispatch(own, ids, weights, cotangent, widths, start, near, capacity):
+    part = start + sum(widths)
     whole = lambda shape: pl.BlockSpec(shape, lambda i, s: (0,) * len(shape))
-    shapes = [(2, capacity, part)] * 2 + [(2, capacity, w) for w in widths] * 2
+    shapes = [(2, capacity, part)] * 2 if near else []
+    shapes = shapes + [(2, capacity, w) for w in widths] * 2
     outs = pl.pallas_call(
-        functools.partial(dispatch_body, start),
+        functools.partial(dispatch_body, start, near),
         grid_spec=pltpu.PrefetchScalarGridSpec(
             num_scalar_prefetch=1,
             grid=(1,),
@@ -121,15 +122,16 @@
             scratch_shapes=[
                 pltpu.VMEM(ids.shape, ids.dtype),
                 pltpu.VMEM(weights.shape, weights.dtype),
-                pltpu.VMEM((tokens, part), cotangent.dtype),
+                pltpu.VMEM((cotangent.shape[0], part), cotangent.dtype),
                 pltpu.SemaphoreType.DMA((3,)),
             ],
         ),
         out_shape=[jax.ShapeDtypeStruct(shape, jnp.bfloat16) for shape in shapes],
-        compiler_params=pltpu.CompilerParams(vmem_limit_bytes=WIDE if start == 0 else NARROW),
+        compiler_params=pltpu.CompilerParams(vmem_limit_bytes=NARROW if near else WIDE),
     )(own, ids, weights, cotangent)
+    near_rows, outs = (outs[:2], outs[2:]) if near else (None, outs)
     n = len(widths)
-    return outs[0], outs[1], outs[2 : 2 + n], outs[2 + n :]
+    return near_rows, outs[:n], outs[n:]
 
 
 def prepare_body(place_ref, hidden_hbm, out_ref, hidden_ref, sems):
@@ -296,25 +298,23 @@
     place = jnp.stack([dp // 8, dp % 4, dp // 4 % 2, own])
     ids, weights = route_ids.T, route_weights.T
     gradients, received = [], []
-    start, turned = 0, None
+    start = 0
     for group, widths in enumerate(GROUPS):
         if group == 1:
-            place, _ = lax.optimization_barrier((place, received[0][1][0]))
+            place, _ = lax.optimization_barrier((place, far[0]))
             turned = prepare(place, hidden)
             own, turned = lax.optimization_barrier((own, turned))
-        mine, partner, far, farther = dispatch(
-            own[None], ids, weights, cotangent, widths, start, capacity
+        rows, far, farther = dispatch(
+            own[None], ids, weights, cotangent, widths, start, group == 1, capacity
         )
-        near = (mine, send(partner, TO_EXPERT[1]))
-        offset = 0
         for index, width in enumerate(widths):
             one = send(far[index], TO_EXPERT[2])
             two = send(farther[index], TO_EXPERT[3])
-            received.append((near, (mine, one, two), offset))
-            offset += width
-        start += sum(widths)
+            received.append(((one, two), start))
+            start += width
+    near = (rows[0], send(rows[1], TO_EXPERT[1]))
     totals = ([], [])
-    for chunk, (near, (_, *far), offset) in enumerate(received):
+    for chunk, (far, offset) in enumerate(received):
         blocks = partials(turned, near, far, offset, RINGS[chunk])
         for local, along in enumerate((ALONG_X, ALONG_Y)):
             (own_block, *sends) = blocks[local]

time: 210 us -> 233 us (1.11)
  the two profiles are of different devices: /device:TPU:102 before, /device:TPU:0 now
where the time goes in v1:
time: 233 us; the launch traced here: 232 us
  waiting for transfers between devices  114 us (49%)
  starting transfers between devices  67.4 us (29%)
  Pallas kernels  36.7 us (16%)
  other arithmetic  8.96 us (4%)
  local copies, waits for them, and re-layouts  3.74 us (2%)
    ppermute x41, waiting for transfers between devices, send(): return lax.ppermute(array, AXES, pairs)  114 us
    ppermute x41, starting transfers between devices, send(): return lax.ppermute(array, AXES, pairs)  67.4 us
    pallas_call x3, Pallas kernels, partials(): pl.pallas_call(functools.partial(matmul_body, ring), grid=(8,), in_specs=...  15.7 us
    pallas_call x1, Pallas kernels, prepare(): pl.pallas_call(prepare_body, grid_spec=pltpu.PrefetchScalarGridSpec(num_s...  10.5 us
    pallas_call x2, Pallas kernels, dispatch(): pl.pallas_call(functools.partial(dispatch_body, start, near), grid_spec=p...  10.4 us
  transfers between devices with their start and end apart: 41, of which 24 were waited for; matrix products, arithmetic and copies ran while one was open for 3% of the time, Pallas kernels for 7%

profile of v1, /device:TPU:0, one launch (start us, length us, event | category | flops | bytes accessed | tf_op | source)
XLA Modules:
  0.0 231.8 jit_solution(17708552805944577557)
XLA Ops:
  0.8 3.8 %shard_map.94 = (bf16[2,192,768]{2,1,0:T(8,128)(2,1)}, bf16[2,192,768]{2,1,0:T(8,128)(2,1)}) custom-call(s32[1]{0:T(128)} %bitcast.3.own_ref, s32[6,1024]{1,0:T(8,128)} %bitcast.23, f32[6,1024]{1,0:T(8,128)} %bitcast.25, bf16[1024,2048]{1,0:T(8,128)(2,1)} %cot_hbm.3), custom_call_target="tpu_custom_call" | custom-call | tf_op jit(solution)/shard_map/pallas_call | solution.py:115
  6.8 10.5 %prepare.1.hidden_ref = bf16[2,1408,768]{2,1,0:T(8,128)(2,1)S(1)} custom-call(s32[4]{0:T(128)S(1)} %pad_add_fusion.place_ref, bf16[2,768,1408]{2,1,0:T(8,128)(2,1)S(1)} %copy-done.1), custom_call_target="tpu_custom_call" | custom-call | tf_op jit(solution)/shard_map/prepare/pallas_call | solution.py:192
  17.4 6.6 %shard_map.95 = (bf16[2,192,2048]{2,1,0:T(8,128)(2,1)S(1)}, bf16[2,192,2048]{2,1,0:T(8,128)(2,1)S(1)}, bf16[2,192,768]{2,1,0:T(8,128)(2,1)S(1)}, bf16[2,192,512]...) custom-call(s32[1]{0:T(128)} %bitcast.6.own_ref, s32[6,1024]{1,0:T(8,128)S(1)} %bitcast.24, ...), custom_call_target="tpu_custom_call" | custom-call | tf_op jit(solution)/shard_map/pallas_call | solution.py:115
  24.1 4.1 %collective-permute-start.6 = (bf16[2,192,768]{2,1,0:T(8,128)(2,1)S(1)}, bf16[2,192,768]{2,1,0:T(8,128)(2,1)S(1)}, u32[]{:S(2)}, u32[]{:S(2)}) collective-permute-start(bf16[2,192,768]{2,1,0:T(8,128)(2,1)S(1)} %get-tuple-element.51), channel_id=1, source_target_pairs={{0,2},{1,3},{16,18},{17,19},{2,0},{3,1},{18,16},{19,17},{4,6},{5,7... | collective-permute-start | bytes 1769480 | tf_op jit(solution)/shard_map/ppermute | solution.py:50
  28.2 3.2 %collective-permute-start.1 = (bf16[2,192,768]{2,1,0:T(8,128)(2,1)S(1)}, bf16[2,192,768]{2,1,0:T(8,128)(2,1)S(1)}, u32[]{:S(2)}, u32[]{:S(2)}) collective-permute-start(bf16[2,192,768]{2,1,0:T(8,128)(2,1)S(1)} %copy-done.8), channel_id=1, source_target_pairs={{0,2},{1,3},{16,18},{17,19},{2,0},{3,1},{18,16},{19,17},{4,6},{5,7... | collective-permute-start | bytes 1769480 | tf_op jit(solution)/shard_map/ppermute | solution.py:50
  31.5 10.8 %collective-permute-done.6.r2 = bf16[2,192,768]{2,1,0:T(8,128)(2,1)S(1)} collective-permute-done((bf16[2,192,768]{2,1,0:T(8,128)(2,1)S(1)}, bf16[2,192,768]{2,1,0:T(8,128)(2,1)S(1)}, u32[]{:S(2)}, u32[]{:S(2)}) %collective-permute-start.6) | collective-permute-done | bytes 589856 | tf_op jit(solution)/shard_map/ppermute | solution.py:50
  42.3 3.5 %collective-permute-start.26 = (bf16[2,192,512]{2,1,0:T(8,128)(2,1)S(1)}, bf16[2,192,512]{2,1,0:T(8,128)(2,1)S(1)}, u32[]{:S(2)}, u32[]{:S(2)}) collective-permute-start(bf16[2,192,512]{2,1,0:T(8,128)(2,1)S(1)} %get-tuple-element.67), channel_id=1, source_target_pairs={{0,2},{1,3},{16,18},{17,19},{2,0},{3,1},{18,16},{19,17},{4,6},{5,7... | collective-permute-start | bytes 1179656 | tf_op jit(solution)/shard_map/ppermute | solution.py:50
  45.9 8.7 %collective-permute-done.7.r3 = bf16[2,192,768]{2,1,0:T(8,128)(2,1)S(1)} collective-permute-done((bf16[2,192,768]{2,1,0:T(8,128)(2,1)S(1)}, bf16[2,192,768]{2,1,0:T(8,128)(2,1)S(1)}, u32[]{:S(2)}, u32[]{:S(2)}) %collective-permute-start.7) | collective-permute-done | bytes 589856 | tf_op jit(solution)/shard_map/ppermute | solution.py:50
  54.5 3.4 %collective-permute-start.27 = (bf16[2,192,512]{2,1,0:T(8,128)(2,1)S(1)}, bf16[2,192,512]{2,1,0:T(8,128)(2,1)S(1)}, u32[]{:S(2)}, u32[]{:S(2)}) collective-permute-start(bf16[2,192,512]{2,1,0:T(8,128)(2,1)S(1)} %get-tuple-element.68), channel_id=1, source_target_pairs={{0,3},{1,2},{16,19},{17,18},{2,1},{3,0},{18,17},{19,16},{4,7},{5,6... | collective-permute-start | bytes 1179656 | tf_op jit(solution)/shard_map/ppermute | solution.py:50
  57.9 5.8 %shard_map.97 = (f32[352,768]{1,0:T(8,128)S(1)}, f32[352,768]{1,0:T(8,128)S(1)}, f32[352,768]{1,0:T(8,128)S(1)}, bf16[176,768]{1,0:T(8,128)(2,1)S(1)}, bf16[176,...) custom-call(bf16[2,1408,768]{2,1,0:T(8,128)(2,1)S(1)} %prepare.1.hid, ...), custom_call_target="tpu_custom_call" | custom-call | tf_op jit(solution)/shard_map/pallas_call | solution.py:241
  67.6 2.8 %collective-permute-start.10 = (bf16[176,768]{1,0:T(8,128)(2,1)S(1)}, bf16[176,768]{1,0:T(8,128)(2,1)S(1)}, u32[]{:S(2)}, u32[]{:S(2)}) collective-permute-start(bf16[176,768]{1,0:T(8,128)(2,1)S(1)} %get-tuple-element.57), channel_id=1, source_target_pairs={{0,96},{1,97},{16,112},{17,113},{2,98},{3,99},{18,114},{19,115},{4... | collective-permute-start | bytes 811016 | tf_op jit(solution)/shard_map/ppermute | solution.py:50
  70.4 9.4 %collective-permute-done.2.r3 = bf16[2,192,768]{2,1,0:T(8,128)(2,1)S(1)} collective-permute-done((bf16[2,192,768]{2,1,0:T(8,128)(2,1)S(1)}, bf16[2,192,768]{2,1,0:T(8,128)(2,1)S(1)}, u32[]{:S(2)}, u32[]{:S(2)}) %collective-permute-start.2) | collective-permute-done | bytes 589856 | tf_op jit(solution)/shard_map/ppermute | solution.py:50
  79.8 5.7 %shard_map.96 = (f32[352,768]{1,0:T(8,128)S(1)}, bf16[352,768]{1,0:T(8,128)(2,1)S(1)}, bf16[352,768]{1,0:T(8,128)(2,1)S(1)}, bf16[352,768]{1,0:T(8,128)(2,1)S(1)...) custom-call(bf16[2,1408,768]{2,1,0:T(8,128)(2,1)S(1)} %prepare.1.hid, ...), custom_call_target="tpu_custom_call" | custom-call | tf_op jit(solution)/shard_map/pallas_call | solution.py:241
  88.7 3.0 %collective-permute-start.4 = (bf16[352,768]{1,0:T(8,128)(2,1)S(1)}, bf16[352,768]{1,0:T(8,128)(2,1)S(1)}, u32[]{:S(2)}, u32[]{:S(2)}) collective-permute-start(bf16[352,768]{1,0:T(8,128)(2,1)S(1)} %get-tuple-element.49), channel_id=1, source_target_pairs={{0,64},{1,65},{16,80},{17,81},{2,66},{3,67},{18,82},{19,83},{4,68}... | collective-permute-start | bytes 1622024 | tf_op jit(solution)/shard_map/ppermute | solution.py:50
  91.7 4.9 %collective-permute-done.27.r3 = bf16[2,192,512]{2,1,0:T(8,128)(2,1)S(1)} collective-permute-done((bf16[2,192,512]{2,1,0:T(8,128)(2,1)S(1)}, bf16[2,192,512]{2,1,0:T(8,128)(2,1)S(1)}, u32[]{:S(2)}, u32[]{:S(2)}) %collective-permute-start.27) | collective-permute-done | bytes 393248 | tf_op jit(solution)/shard_map/ppermute | solution.py:50
  98.1 4.3 %shard_map.98 = (f32[352,512]{1,0:T(8,128)S(1)}, bf16[352,512]{1,0:T(8,128)(2,1)S(1)}, bf16[352,512]{1,0:T(8,128)(2,1)S(1)}, bf16[352,512]{1,0:T(8,128)(2,1)S(1)...) custom-call(bf16[2,1408,768]{2,1,0:T(8,128)(2,1)S(1)} %prepare.1.hid, ...), custom_call_target="tpu_custom_call" | custom-call | tf_op jit(solution)/shard_map/pallas_call | solution.py:241
  106.3 3.0 %collective-permute-start.29 = (bf16[352,512]{1,0:T(8,128)(2,1)S(1)}, bf16[352,512]{1,0:T(8,128)(2,1)S(1)}, u32[]{:S(2)}, u32[]{:S(2)}) collective-permute-start(bf16[352,512]{1,0:T(8,128)(2,1)S(1)} %get-tuple-element.71), channel_id=1, source_target_pairs={{0,64},{1,65},{16,80},{17,81},{2,66},{3,67},{18,82},{19,83},{4,68}... | collective-permute-start | bytes 1081352 | tf_op jit(solution)/shard_map/ppermute | solution.py:50
  110.7 3.0 %collective-permute-start.30 = (bf16[352,512]{1,0:T(8,128)(2,1)S(1)}, bf16[352,512]{1,0:T(8,128)(2,1)S(1)}, u32[]{:S(2)}, u32[]{:S(2)}) collective-permute-start(bf16[352,512]{1,0:T(8,128)(2,1)S(1)} %get-tuple-element.72), channel_id=1, source_target_pairs={{0,96},{1,97},{16,112},{17,113},{2,98},{3,99},{18,114},{19,115},{4... | collective-permute-start | bytes 1081352 | tf_op jit(solution)/shard_map/ppermute | solution.py:50
  114.0 8.2 %collective-permute-done.28 = bf16[352,512]{1,0:T(8,128)(2,1)S(1)} collective-permute-done((bf16[352,512]{1,0:T(8,128)(2,1)S(1)}, bf16[352,512]{1,0:T(8,128)(2,1)S(1)}, u32[]{:S(2)}, u32[]{:S(2)}) %collective-permute-start.28) | collective-permute-done | bytes 360480 | tf_op jit(solution)/shard_map/ppermute | solution.py:50
  123.7 5.6 %collective-permute-done.29 = bf16[352,512]{1,0:T(8,128)(2,1)S(1)} collective-permute-done((bf16[352,512]{1,0:T(8,128)(2,1)S(1)}, bf16[352,512]{1,0:T(8,128)(2,1)S(1)}, u32[]{:S(2)}, u32[]{:S(2)}) %collective-permute-start.29) | collective-permute-done | bytes 360480 | tf_op jit(solution)/shard_map/ppermute | solution.py:50
  129.3 3.2 %collective-permute-start.35 = (bf16[352,512]{1,0:T(8,128)(2,1)S(1)}, bf16[352,512]{1,0:T(8,128)(2,1)S(1)}, u32[]{:S(2)}, u32[]{:S(2)}) collective-permute-start(bf16[352,512]{1,0:T(8,128)(2,1)S(1)} %get-tuple-element.75), channel_id=1, source_target_pairs={{0,8},{1,9},{16,24},{17,25},{2,10},{3,11},{18,26},{19,27},{4,12},{... | collective-permute-start | bytes 1081352 | tf_op jit(solution)/shard_map/ppermute | solution.py:50
  134.8 8.7 %collective-permute-done.35 = bf16[352,512]{1,0:T(8,128)(2,1)S(1)} collective-permute-done((bf16[352,512]{1,0:T(8,128)(2,1)S(1)}, bf16[352,512]{1,0:T(8,128)(2,1)S(1)}, u32[]{:S(2)}, u32[]{:S(2)}) %collective-permute-start.35) | collective-permute-done | bytes 360480 | tf_op jit(solution)/shard_map/ppermute | solution.py:50
  144.8 4.9 %collective-permute-done.36 = bf16[352,512]{1,0:T(8,128)(2,1)S(1)} collective-permute-done((bf16[352,512]{1,0:T(8,128)(2,1)S(1)}, bf16[352,512]{1,0:T(8,128)(2,1)S(1)}, u32[]{:S(2)}, u32[]{:S(2)}) %collective-permute-start.36) | collective-permute-done | bytes 360480 | tf_op jit(solution)/shard_map/ppermute | solution.py:50
  156.1 3.9 %collective-permute-done.37 = f16[88,512]{1,0:T(8,128)(2,1)S(1)} collective-permute-done((f16[88,512]{1,0:T(8,128)(2,1)S(1)}, f16[88,512]{1,0:T(8,128)(2,1)S(1)}, u32[]{:S(2)}, u32[]{:S(2)}) %collective-permute-start.37) | collective-permute-done | bytes 90144 | tf_op jit(solution)/shard_map/ppermute | solution.py:50
  166.1 7.7 %collective-permute-done.5 = bf16[352,768]{1,0:T(8,128)(2,1)S(1)} collective-permute-done((bf16[352,768]{1,0:T(8,128)(2,1)S(1)}, bf16[352,768]{1,0:T(8,128)(2,1)S(1)}, u32[]{:S(2)}, u32[]{:S(2)}) %collective-permute-start.5) | collective-permute-done | bytes 540704 | tf_op jit(solution)/shard_map/ppermute | solution.py:50
  175.5 11.1 %collective-permute-done.15 = bf16[352,768]{1,0:T(8,128)(2,1)S(1)} collective-permute-done((bf16[352,768]{1,0:T(8,128)(2,1)S(1)}, bf16[352,768]{1,0:T(8,128)(2,1)S(1)}, u32[]{:S(2)}, u32[]{:S(2)}) %collective-permute-start.15) | collective-permute-done | bytes 540704 | tf_op jit(solution)/shard_map/ppermute | solution.py:50
  186.6 3.2 %collective-permute-start.21 = (f16[352,768]{1,0:T(8,128)(2,1)S(1)}, f16[352,768]{1,0:T(8,128)(2,1)S(1)}, u32[]{:S(2)}, u32[]{:S(2)}) collective-permute-start(f16[352,768]{1,0:T(8,128)(2,1)S(1)} %fusion.3), channel_id=1, source_target_pairs={{0,12},{1,13},{16,28},{17,29},{2,14},{3,15},{18,30},{19,31},{4,0},... | collective-permute-start | bytes 1622024 | tf_op jit(solution)/shard_map/ppermute | solution.py:50
  194.1 10.7 %collective-permute-done.19 = f16[352,768]{1,0:T(8,128)(2,1)S(1)} collective-permute-done((f16[352,768]{1,0:T(8,128)(2,1)S(1)}, f16[352,768]{1,0:T(8,128)(2,1)S(1)}, u32[]{:S(2)}, u32[]{:S(2)}) %collective-permute-start.19) | collective-permute-done | bytes 540704 | tf_op jit(solution)/shard_map/ppermute | solution.py:50
  211.1 3.5 %collective-permute-start.24 = (f16[88,1536]{1,0:T(8,128)(2,1)S(1)}, f16[88,1536]{1,0:T(8,128)(2,1)S(1)}, u32[]{:S(2)}, u32[]{:S(2)}) collective-permute-start(f16[88,1536]{1,0:T(8,128)(2,1)S(1)} %get-tuple-element.84), channel_id=1, source_target_pairs={{0,96},{1,97},{16,112},{17,113},{2,98},{3,99},{18,114},{19,115},{4... | collective-permute-start | bytes 811016 | tf_op jit(solution)/shard_map/ppermute | solution.py:50
  215.6 3.4 %collective-permute-done.23 = f16[88,1536]{1,0:T(8,128)(2,1)S(1)} collective-permute-done((f16[88,1536]{1,0:T(8,128)(2,1)S(1)}, f16[88,1536]{1,0:T(8,128)(2,1)S(1)}, u32[]{:S(2)}, u32[]{:S(2)}) %collective-permute-start.23) | collective-permute-done | bytes 270368 | tf_op jit(solution)/shard_map/ppermute | solution.py:50
  223.7 3.6 %collective-permute-done.25 = f16[2,44,1536]{2,0,1:T(2,128)(2,1)S(1)} collective-permute-done((f16[2,44,1536]{2,0,1:T(2,128)(2,1)S(1)}, f16[2,44,1536]{2,0,1:T(2,128)(2,1)S(1)}, u32[]{:S(2)}, u32[]{:S(2)}) %collective-permute-start.25) | collective-permute-done | bytes 270368 | tf_op jit(solution)/shard_map/ppermute | solution.py:50
  227.9 3.8 %multiply_subtract_fusion = (f32[44,2,2048]{2,1,0:T(2,128)}, f32[44,2,2048]{2,1,0:T(2,128)}, f32[44,2,2048]{2,1,0:T(2,128)}) fusion(f32[44,2,2048]{2,1,0:T(2,128)S(1)} %copy-done.4, f32[44,2,512]{2,1,0:T(2,128)S(1)} %fusion.41, f32[44,2,1536]{2,1,0:T(2,128)S(1)} %fusion.28, f32[44,2,2048]{2,1,0:T(2,128)S(1)} %copy-done.5, f32[44,2,2048]{2,1,0:T(2,128)S(1)} %copy-done.6), kind=kLoop, calls=%fused_computation.25 | loop fusion | flops 3063808 | bytes 5046272 | tf_op jit(solution)/shard_map/sub | solution.py:344
  (114 shorter events, 52.5 us)
Async XLA Ops:
  24.0 33.9 %collective-permute-start = (bf16[2,192,2048]{2,1,0:T(8,128)(2,1)S(1)}, bf16[2,192,2048]{2,1,0:T(8,128)(2,1)S(1)}, u32[]{:S(2)}, u32[]{:S(2)}) collective-permute-start(bf16[2,192,2048]{2,1,0:T(8,128)(2,1)S(1)} %get-tuple-element.45), channel_id=1, source_target_pairs={{0,1},{1,0},{16,17},{17,16},{2,3},{3,2},{18,19},{19,18},{4,5},{5,4... | collective-permute-start | bytes 4718600 | tf_op jit(solution)/shard_map/ppermute | solution.py:50
  24.1 18.2 %collective-permute-start.6 = (bf16[2,192,768]{2,1,0:T(8,128)(2,1)S(1)}, bf16[2,192,768]{2,1,0:T(8,128)(2,1)S(1)}, u32[]{:S(2)}, u32[]{:S(2)}) collective-permute-start(bf16[2,192,768]{2,1,0:T(8,128)(2,1)S(1)} %get-tuple-element.51), channel_id=1, source_target_pairs={{0,2},{1,3},{16,18},{17,19},{2,0},{3,1},{18,16},{19,17},{4,6},{5,7... | collective-permute-start | bytes 1769480 | tf_op jit(solution)/shard_map/ppermute | solution.py:50
  28.1 26.4 %collective-permute-start.7 = (bf16[2,192,768]{2,1,0:T(8,128)(2,1)S(1)}, bf16[2,192,768]{2,1,0:T(8,128)(2,1)S(1)}, u32[]{:S(2)}, u32[]{:S(2)}) collective-permute-start(bf16[2,192,768]{2,1,0:T(8,128)(2,1)S(1)} %get-tuple-element.52), channel_id=1, source_target_pairs={{0,3},{1,2},{16,19},{17,18},{2,1},{3,0},{18,17},{19,16},{4,7},{5,6... | collective-permute-start | bytes 1769480 | tf_op jit(solution)/shard_map/ppermute | solution.py:50
  28.2 39.4 %collective-permute-start.1 = (bf16[2,192,768]{2,1,0:T(8,128)(2,1)S(1)}, bf16[2,192,768]{2,1,0:T(8,128)(2,1)S(1)}, u32[]{:S(2)}, u32[]{:S(2)}) collective-permute-start(bf16[2,192,768]{2,1,0:T(8,128)(2,1)S(1)} %copy-done.8), channel_id=1, source_target_pairs={{0,2},{1,3},{16,18},{17,19},{2,0},{3,1},{18,16},{19,17},{4,6},{5,7... | collective-permute-start | bytes 1769480 | tf_op jit(solution)/shard_map/ppermute | solution.py:50
  31.4 48.4 %collective-permute-start.2 = (bf16[2,192,768]{2,1,0:T(8,128)(2,1)S(1)}, bf16[2,192,768]{2,1,0:T(8,128)(2,1)S(1)}, u32[]{:S(2)}, u32[]{:S(2)}) collective-permute-start(bf16[2,192,768]{2,1,0:T(8,128)(2,1)S(1)} %copy-done.7), channel_id=1, source_target_pairs={{0,3},{1,2},{16,19},{17,18},{2,1},{3,0},{18,17},{19,16},{4,7},{5,6... | collective-permute-start | bytes 1769480 | tf_op jit(solution)/shard_map/ppermute | solution.py:50
  42.3 46.3 %collective-permute-start.26 = (bf16[2,192,512]{2,1,0:T(8,128)(2,1)S(1)}, bf16[2,192,512]{2,1,0:T(8,128)(2,1)S(1)}, u32[]{:S(2)}, u32[]{:S(2)}) collective-permute-start(bf16[2,192,512]{2,1,0:T(8,128)(2,1)S(1)} %get-tuple-element.67), channel_id=1, source_target_pairs={{0,2},{1,3},{16,18},{17,19},{2,0},{3,1},{18,16},{19,17},{4,6},{5,7... | collective-permute-start | bytes 1179656 | tf_op jit(solution)/shard_map/ppermute | solution.py:50
  54.5 42.0 %collective-permute-start.27 = (bf16[2,192,512]{2,1,0:T(8,128)(2,1)S(1)}, bf16[2,192,512]{2,1,0:T(8,128)(2,1)S(1)}, u32[]{:S(2)}, u32[]{:S(2)}) collective-permute-start(bf16[2,192,512]{2,1,0:T(8,128)(2,1)S(1)} %get-tuple-element.68), channel_id=1, source_target_pairs={{0,3},{1,2},{16,19},{17,18},{2,1},{3,0},{18,17},{19,16},{4,7},{5,6... | collective-permute-start | bytes 1179656 | tf_op jit(solution)/shard_map/ppermute | solution.py:50
  63.7 38.7 %collective-permute-start.8 = (bf16[176,768]{1,0:T(8,128)(2,1)S(1)}, bf16[176,768]{1,0:T(8,128)(2,1)S(1)}, u32[]{:S(2)}, u32[]{:S(2)}) collective-permute-start(bf16[176,768]{1,0:T(8,128)(2,1)S(1)} %get-tuple-element.55), channel_id=1, source_target_pairs={{0,32},{1,33},{16,48},{17,49},{2,34},{3,35},{18,50},{19,51},{4,36}... | collective-permute-start | bytes 811016 | tf_op jit(solution)/shard_map/ppermute | solution.py:50
  67.6 36.7 %collective-permute-start.10 = (bf16[176,768]{1,0:T(8,128)(2,1)S(1)}, bf16[176,768]{1,0:T(8,128)(2,1)S(1)}, u32[]{:S(2)}, u32[]{:S(2)}) collective-permute-start(bf16[176,768]{1,0:T(8,128)(2,1)S(1)} %get-tuple-element.57), channel_id=1, source_target_pairs={{0,96},{1,97},{16,112},{17,113},{2,98},{3,99},{18,114},{19,115},{4... | collective-permute-start | bytes 811016 | tf_op jit(solution)/shard_map/ppermute | solution.py:50
  85.5 76.4 %collective-permute-start.3 = (bf16[352,768]{1,0:T(8,128)(2,1)S(1)}, bf16[352,768]{1,0:T(8,128)(2,1)S(1)}, u32[]{:S(2)}, u32[]{:S(2)}) collective-permute-start(bf16[352,768]{1,0:T(8,128)(2,1)S(1)} %get-tuple-element.48), channel_id=1, source_target_pairs={{0,32},{1,33},{16,48},{17,49},{2,34},{3,35},{18,50},{19,51},{4,36}... | collective-permute-start | bytes 1622024 | tf_op jit(solution)/shard_map/ppermute | solution.py:50
  88.7 75.3 %collective-permute-start.4 = (bf16[352,768]{1,0:T(8,128)(2,1)S(1)}, bf16[352,768]{1,0:T(8,128)(2,1)S(1)}, u32[]{:S(2)}, u32[]{:S(2)}) collective-permute-start(bf16[352,768]{1,0:T(8,128)(2,1)S(1)} %get-tuple-element.49), channel_id=1, source_target_pairs={{0,64},{1,65},{16,80},{17,81},{2,66},{3,67},{18,82},{19,83},{4,68}... | collective-permute-start | bytes 1622024 | tf_op jit(solution)/shard_map/ppermute | solution.py:50
  96.5 9.8 %collective-permute-start.18 = (bf16[176,768]{1,0:T(8,128)(2,1)S(1)}, bf16[176,768]{1,0:T(8,128)(2,1)S(1)}, u32[]{:S(2)}, u32[]{:S(2)}) collective-permute-start(bf16[176,768]{1,0:T(8,128)(2,1)S(1)} %get-tuple-element.64), channel_id=1, source_target_pairs={{0,4},{1,5},{16,20},{17,21},{2,6},{3,7},{18,22},{19,23},{4,8},{5,9... | collective-permute-start | bytes 811016 | tf_op jit(solution)/shard_map/ppermute | solution.py:50
  104.3 17.9 %collective-permute-start.28 = (bf16[352,512]{1,0:T(8,128)(2,1)S(1)}, bf16[352,512]{1,0:T(8,128)(2,1)S(1)}, u32[]{:S(2)}, u32[]{:S(2)}) collective-permute-start(bf16[352,512]{1,0:T(8,128)(2,1)S(1)} %get-tuple-element.70), channel_id=1, source_target_pairs={{0,32},{1,33},{16,48},{17,49},{2,34},{3,35},{18,50},{19,51},{4,36}... | collective-permute-start | bytes 1081352 | tf_op jit(solution)/shard_map/ppermute | solution.py:50
  106.3 23.0 %collective-permute-start.29 = (bf16[352,512]{1,0:T(8,128)(2,1)S(1)}, bf16[352,512]{1,0:T(8,128)(2,1)S(1)}, u32[]{:S(2)}, u32[]{:S(2)}) collective-permute-start(bf16[352,512]{1,0:T(8,128)(2,1)S(1)} %get-tuple-element.71), channel_id=1, source_target_pairs={{0,64},{1,65},{16,80},{17,81},{2,66},{3,67},{18,82},{19,83},{4,68}... | collective-permute-start | bytes 1081352 | tf_op jit(solution)/shard_map/ppermute | solution.py:50
  110.7 21.7 %collective-permute-start.30 = (bf16[352,512]{1,0:T(8,128)(2,1)S(1)}, bf16[352,512]{1,0:T(8,128)(2,1)S(1)}, u32[]{:S(2)}, u32[]{:S(2)}) collective-permute-start(bf16[352,512]{1,0:T(8,128)(2,1)S(1)} %get-tuple-element.72), channel_id=1, source_target_pairs={{0,96},{1,97},{16,112},{17,113},{2,98},{3,99},{18,114},{19,115},{4... | collective-permute-start | bytes 1081352 | tf_op jit(solution)/shard_map/ppermute | solution.py:50
  122.2 11.6 %collective-permute-start.34 = (bf16[352,512]{1,0:T(8,128)(2,1)S(1)}, bf16[352,512]{1,0:T(8,128)(2,1)S(1)}, u32[]{:S(2)}, u32[]{:S(2)}) collective-permute-start(bf16[352,512]{1,0:T(8,128)(2,1)S(1)} %get-tuple-element.74), channel_id=1, source_target_pairs={{0,4},{1,5},{16,20},{17,21},{2,6},{3,7},{18,22},{19,23},{4,8},{5,9... | collective-permute-start | bytes 1081352 | tf_op jit(solution)/shard_map/ppermute | solution.py:50
  129.3 14.3 %collective-permute-start.35 = (bf16[352,512]{1,0:T(8,128)(2,1)S(1)}, bf16[352,512]{1,0:T(8,128)(2,1)S(1)}, u32[]{:S(2)}, u32[]{:S(2)}) collective-permute-start(bf16[352,512]{1,0:T(8,128)(2,1)S(1)} %get-tuple-element.75), channel_id=1, source_target_pairs={{0,8},{1,9},{16,24},{17,25},{2,10},{3,11},{18,26},{19,27},{4,12},{... | collective-permute-start | bytes 1081352 | tf_op jit(solution)/shard_map/ppermute | solution.py:50
  132.5 17.1 %collective-permute-start.36 = (bf16[352,512]{1,0:T(8,128)(2,1)S(1)}, bf16[352,512]{1,0:T(8,128)(2,1)S(1)}, u32[]{:S(2)}, u32[]{:S(2)}) collective-permute-start(bf16[352,512]{1,0:T(8,128)(2,1)S(1)} %get-tuple-element.76), channel_id=1, source_target_pairs={{0,12},{1,13},{16,28},{17,29},{2,14},{3,15},{18,30},{19,31},{4,0},... | collective-permute-start | bytes 1081352 | tf_op jit(solution)/shard_map/ppermute | solution.py:50
  133.8 18.7 %collective-permute-start.31 = (f16[88,512]{1,0:T(8,128)(2,1)S(1)}, f16[88,512]{1,0:T(8,128)(2,1)S(1)}, u32[]{:S(2)}, u32[]{:S(2)}) collective-permute-start(f16[88,512]{1,0:T(8,128)(2,1)S(1)} %get-tuple-element.94), channel_id=1, source_target_pairs={{0,4},{1,5},{16,20},{17,21},{2,6},{3,7},{18,22},{19,23},{4,8},{5,9... | collective-permute-start | bytes 270344 | tf_op jit(solution)/shard_map/ppermute | solution.py:50
  143.6 9.0 %collective-permute-start.32 = (f16[88,512]{1,0:T(8,128)(2,1)S(1)}, f16[88,512]{1,0:T(8,128)(2,1)S(1)}, u32[]{:S(2)}, u32[]{:S(2)}) collective-permute-start(f16[88,512]{1,0:T(8,128)(2,1)S(1)} %get-tuple-element.96), channel_id=1, source_target_pairs={{0,8},{1,9},{16,24},{17,25},{2,10},{3,11},{18,26},{19,27},{4,12},{... | collective-permute-start | bytes 270344 | tf_op jit(solution)/shard_map/ppermute | solution.py:50
  160.0 13.8 %collective-permute-start.5 = (bf16[352,768]{1,0:T(8,128)(2,1)S(1)}, bf16[352,768]{1,0:T(8,128)(2,1)S(1)}, u32[]{:S(2)}, u32[]{:S(2)}) collective-permute-start(bf16[352,768]{1,0:T(8,128)(2,1)S(1)} %get-tuple-element.50), channel_id=1, source_target_pairs={{0,96},{1,97},{16,112},{17,113},{2,98},{3,99},{18,114},{19,115},{4... | collective-permute-start | bytes 1622024 | tf_op jit(solution)/shard_map/ppermute | solution.py:50
  160.0 26.6 %collective-permute-start.15 = (bf16[352,768]{1,0:T(8,128)(2,1)S(1)}, bf16[352,768]{1,0:T(8,128)(2,1)S(1)}, u32[]{:S(2)}, u32[]{:S(2)}) collective-permute-start(bf16[352,768]{1,0:T(8,128)(2,1)S(1)} %get-tuple-element.59), channel_id=1, source_target_pairs={{0,4},{1,5},{16,20},{17,21},{2,6},{3,7},{18,22},{19,23},{4,8},{5,9... | collective-permute-start | bytes 1622024 | tf_op jit(solution)/shard_map/ppermute | solution.py:50
  160.6 26.0 %collective-permute-start.16 = (bf16[352,768]{1,0:T(8,128)(2,1)S(1)}, bf16[352,768]{1,0:T(8,128)(2,1)S(1)}, u32[]{:S(2)}, u32[]{:S(2)}) collective-permute-start(bf16[352,768]{1,0:T(8,128)(2,1)S(1)} %get-tuple-element.60), channel_id=1, source_target_pairs={{0,8},{1,9},{16,24},{17,25},{2,10},{3,11},{18,26},{19,27},{4,12},{... | collective-permute-start | bytes 1622024 | tf_op jit(solution)/shard_map/ppermute | solution.py:50
  161.9 28.0 %collective-permute-start.17 = (bf16[352,768]{1,0:T(8,128)(2,1)S(1)}, bf16[352,768]{1,0:T(8,128)(2,1)S(1)}, u32[]{:S(2)}, u32[]{:S(2)}) collective-permute-start(bf16[352,768]{1,0:T(8,128)(2,1)S(1)} %get-tuple-element.61), channel_id=1, source_target_pairs={{0,12},{1,13},{16,28},{17,29},{2,14},{3,15},{18,30},{19,31},{4,0},... | collective-permute-start | bytes 1622024 | tf_op jit(solution)/shard_map/ppermute | solution.py:50
  164.0 28.1 %collective-permute-start.9 = (f16[352,768]{1,0:T(8,128)(2,1)S(1)}, f16[352,768]{1,0:T(8,128)(2,1)S(1)}, u32[]{:S(2)}, u32[]{:S(2)}) collective-permute-start(f16[352,768]{1,0:T(8,128)(2,1)S(1)} %fusion), channel_id=1, source_target_pairs={{0,32},{1,33},{16,48},{17,49},{2,34},{3,35},{18,50},{19,51},{4,36}... | collective-permute-start | bytes 1622024 | tf_op jit(solution)/shard_map/ppermute | solution.py:50
  173.8 18.3 %collective-permute-start.11 = (f16[352,768]{1,0:T(8,128)(2,1)S(1)}, f16[352,768]{1,0:T(8,128)(2,1)S(1)}, u32[]{:S(2)}, u32[]{:S(2)}) collective-permute-start(f16[352,768]{1,0:T(8,128)(2,1)S(1)} %fusion.1), channel_id=1, source_target_pairs={{0,96},{1,97},{16,112},{17,113},{2,98},{3,99},{18,114},{19,115},{4... | collective-permute-start | bytes 1622024 | tf_op jit(solution)/shard_map/ppermute | solution.py:50
  186.6 18.2 %collective-permute-start.19 = (f16[352,768]{1,0:T(8,128)(2,1)S(1)}, f16[352,768]{1,0:T(8,128)(2,1)S(1)}, u32[]{:S(2)}, u32[]{:S(2)}) collective-permute-start(f16[352,768]{1,0:T(8,128)(2,1)S(1)} %fusion.2), channel_id=1, source_target_pairs={{0,4},{1,5},{16,20},{17,21},{2,6},{3,7},{18,22},{19,23},{4,8},{5,9... | collective-permute-start | bytes 1622024 | tf_op jit(solution)/shard_map/ppermute | solution.py:50
  186.6 20.9 %collective-permute-start.21 = (f16[352,768]{1,0:T(8,128)(2,1)S(1)}, f16[352,768]{1,0:T(8,128)(2,1)S(1)}, u32[]{:S(2)}, u32[]{:S(2)}) collective-permute-start(f16[352,768]{1,0:T(8,128)(2,1)S(1)} %fusion.3), channel_id=1, source_target_pairs={{0,12},{1,13},{16,28},{17,29},{2,14},{3,15},{18,30},{19,31},{4,0},... | collective-permute-start | bytes 1622024 | tf_op jit(solution)/shard_map/ppermute | solution.py:50
  189.8 33.1 %collective-permute-start.40 = (f16[2,44,512]{2,0,1:T(2,128)(2,1)S(1)}, f16[2,44,512]{2,0,1:T(2,128)(2,1)S(1)}, u32[]{:S(2)}, u32[]{:S(2)}) collective-permute-start(f16[2,44,512]{2,0,1:T(2,128)(2,1)S(1)} %pad_maximum_fusion.4), channel_id=1, source_target_pairs={{0,16},{1,17},{16,0},{17,1},{2,18},{3,19},{18,2},{19,3},{4,20},{5,... | collective-permute-start | bytes 270344 | tf_op jit(solution)/shard_map/ppermute | solution.py:50
  192.5 18.6 %collective-permute-start.12 = (f16[88,1536]{1,0:T(8,128)(2,1)S(1)}, f16[88,1536]{1,0:T(8,128)(2,1)S(1)}, u32[]{:S(2)}, u32[]{:S(2)}) collective-permute-start(f16[88,1536]{1,0:T(8,128)(2,1)S(1)} %get-tuple-element.80), channel_id=1, source_target_pairs={{0,4},{1,5},{16,20},{17,21},{2,6},{3,7},{18,22},{19,23},{4,8},{5,9... | collective-permute-start | bytes 811016 | tf_op jit(solution)/shard_map/ppermute | solution.py:50
  192.6 18.5 %collective-permute-start.13 = (f16[88,1536]{1,0:T(8,128)(2,1)S(1)}, f16[88,1536]{1,0:T(8,128)(2,1)S(1)}, u32[]{:S(2)}, u32[]{:S(2)}) collective-permute-start(f16[88,1536]{1,0:T(8,128)(2,1)S(1)} %get-tuple-element.82), channel_id=1, source_target_pairs={{0,8},{1,9},{16,24},{17,25},{2,10},{3,11},{18,26},{19,27},{4,12},{... | collective-permute-start | bytes 811016 | tf_op jit(solution)/shard_map/ppermute | solution.py:50
  204.8 9.7 %collective-permute-start.14 = (f16[88,1536]{1,0:T(8,128)(2,1)S(1)}, f16[88,1536]{1,0:T(8,128)(2,1)S(1)}, u32[]{:S(2)}, u32[]{:S(2)}) collective-permute-start(f16[88,1536]{1,0:T(8,128)(2,1)S(1)} %get-tuple-element.81), channel_id=1, source_target_pairs={{0,12},{1,13},{16,28},{17,29},{2,14},{3,15},{18,30},{19,31},{4,0},... | collective-permute-start | bytes 811016 | tf_op jit(solution)/shard_map/ppermute | solution.py:50
  (18 other events, 136.9 us)
